TPU v7x, 32 devices: a whole 2x2x4 slice. The times are simulated.
32 devices in a mesh: seq: 16 (over z, y, core), fsdp: 2 (over x).
Axes of the slice: x: 2, y: 2, z: 4, core: 2. Of those that a mesh axis runs over, the one named last changes fastest.
Arguments:
- residual: bfloat16 [2, 1024, 1440], P('fsdp', 'seq'), may hold values from -40 to 40
- queries: bfloat16 [2, 1024, 2048], P('fsdp', 'seq'), may hold values from -64 to 64
- key_rows: bfloat16 [2, 1024, 256], P('fsdp', 'seq'), may hold values from -16 to 16
- values: bfloat16 [2, 1024, 256], P('fsdp', 'seq'), may hold values from -1 to 2
- attention_sinks: float32 [32], replicated, may hold values from 0 to 6
- out_weight: bfloat16 [2048, 1440], P('seq', 'fsdp'), may hold values from -0.125 to 0.125
- norm_gain: bfloat16 [1440], replicated, may hold values from 0.25 to 1.75
- router_weight: bfloat16 [1440, 16], replicated, may hold values from -0.15625 to 0.15625
- gate_weight: bfloat16 [1440, 23040], P(None, 'seq'), may hold values from -0.15625 to 0.15625
- up_weight: bfloat16 [1440, 23040], P(None, 'seq'), may hold values from -0.15625 to 0.15625
- down_weight: bfloat16 [23040, 1440], P('seq'), may hold values from -0.15625 to 0.15625
- routing: int32 [2, 1024, 2], P('fsdp', 'seq'), may hold values from 0 to 15, as said below
- span_order: int32 [32], replicated, may hold values from 0 to 31, as said below
Outputs:
- attended: bfloat16 [2, 1024, 1440], P('fsdp', 'seq')
- layer_output: bfloat16 [2, 1024, 1440], P('fsdp', 'seq')
Inputs may be any that keep to these rules, and one draw needn't show every extreme that they name: A permutation of 0 to 31; index i of seq holds the rows of spans span_order[2 i] and span_order[2 i + 1], and these two add up to 31. `routing`: in the rows of one device no expert is named more than 12 times; in each prompt one expert is named exactly 12 times in the rows of every device; the 2 experts of a row differ.
All inputs are finite; a program needn't handle non-finite values.
Results may differ from a plain program's by a relative error of at most 0.009.
Values may be sent and summed in bfloat16 or wider, within the bound.
A program may use at most 64 MiB of HBM per device.

v0:
```python
import functools

import jax
import jax.numpy as jnp
from jax import lax
from jax.experimental import pallas as pl
from jax.experimental.pallas import tpu as pltpu
from jax.sharding import PartitionSpec as P

D = 1440
HEADS = 32
KVH = 4
HD = 64
EXPERTS = 16
TOPK = 2
TOK_DEV = 64
HALF = 32
CAP = 12


rope_base = 150000.0
norm_eps = 1e-05
masked_score = -1e30


MESH = pl.DeviceIdType.MESH


def remote(source, target, send_sem, recv_sem, **where):
    return pltpu.make_async_remote_copy(
        src_ref=source,
        dst_ref=target,
        send_sem=send_sem,
        recv_sem=recv_sem,
        device_id=where,
        device_id_type=MESH,
    )


def greet(peers):
    barrier = pltpu.get_barrier_semaphore()
    for where in peers:
        pl.semaphore_signal(barrier, inc=1, device_id=where, device_id_type=MESH)
    pl.semaphore_wait(barrier, len(peers))


def gather_plan(block, slots, sems, z_count, z, y, c):
    z_send, z_recv, y_send, y_recv, c_send, c_recv, own_sem = sems

    def slot(zz, yy, cc):
        return (zz * 2 + yy) * 2 + cc

    def z_of(d):
        return lax.rem(z + z_count - d, z_count)

    own = slot(z, y, c)
    to_z = [
        remote(block, slots.at[own], z_send.at[d], z_recv.at[d], seq=slot(lax.rem(z + d, z_count), y, c))
        for d in range(1, z_count)
    ]

    def to_y(d):
        source = block if d == 0 else slots.at[slot(z_of(d), y, c)]
        return remote(source, slots.at[slot(z_of(d), y, c)], y_send.at[d], y_recv.at[d], seq=slot(z, 1 - y, c))

    def to_c(side, d):
        index = slot(z_of(d), y if side == 0 else 1 - y, c)
        source = block if side == 0 and d == 0 else slots.at[index]
        return remote(source, slots.at[index], c_send.at[side, d], c_recv.at[side, d], seq=slot(z, y, 1 - c))

    local = pltpu.make_async_copy(block, slots.at[own], own_sem)
    ys = [to_y(d) for d in range(z_count)]
    cs = [[to_c(side, d) for d in range(z_count)] for side in range(2)]

    def start_z():
        local.start()
        for copy in to_z:
            copy.start()

    def relay(d):
        if d > 0:
            to_z[d - 1].wait_recv()
        ys[d].start()
        cs[0][d].start()

    def relay_across(d):
        ys[d].wait_recv()
        cs[1][d].start()

    def finish():
        for side in range(2):
            for d in range(z_count):
                cs[side][d].wait_recv()
        local.wait()

    def drain():
        for copy in to_z + ys + cs[0] + cs[1]:
            copy.wait_send()

    return start_z, relay, relay_across, finish, drain


def layer_kernel(
    seq_count, fsdp_count,
    sink_ref, span_ref, gain_ref, routing_ref,
    res_hbm, q_hbm, k_hbm, v_hbm, w_hbm, router_hbm, gate_hbm, up_hbm, down_hbm,
    attended_ref, layer_ref,
    res, q_raw, k_raw, v_raw, router, gate, up, down,
    kv_own, kv_all, w_own, w_all, q_rot, bias, rows_all, proj, got,
    x_out, arrived, stacked, back, returned, restacked,
    load_sems,
    kzs, kzr, kys, kyr, kcs, kcr, wzs, wzr, wys, wyr, wcs, wcr, own_sems, as_, ar, ps, pr,
    xs, xr, bs, br,
):
    sources = (k_hbm, v_hbm, w_hbm, q_hbm, res_hbm, router_hbm, gate_hbm, up_hbm, down_hbm)
    targets = (k_raw, v_raw, w_own, q_raw, res, router, gate, up, down)
    loads = [
        pltpu.make_async_copy(a, b, load_sems.at[i]) for i, (a, b) in enumerate(zip(sources, targets))
    ]
    for load in loads[:6]:
        load.start()

    me = lax.axis_index("seq")
    f_me = lax.axis_index("fsdp")
    z_count = seq_count // 4
    z, y, c = me // 4, lax.rem(me // 2, 2), lax.rem(me, 2)
    rows, key_count = bias.shape
    group_size = HEADS // KVH
    copies = seq_count // EXPERTS

    def spot(row):
        return jnp.where(row < HALF, span_ref[0, 2 * me], span_ref[0, 2 * me + 1]) * HALF + row % HALF

    lane = lax.broadcasted_iota(jnp.int32, (rows, 2 * HD), 1)
    place = spot(lax.broadcasted_iota(jnp.int32, (rows, 2 * HD), 0)).astype(jnp.float32)
    half = HD // 2
    frequency = jnp.exp(-jnp.log(rope_base) * (lane % half).astype(jnp.float32) / half)
    angles = place * frequency
    low = (lane % HD) < half
    cosine = jnp.cos(angles)
    sine = jnp.where(low, -jnp.sin(angles), jnp.sin(angles))

    def rotated(pair):
        x = pair.astype(jnp.float32)
        swapped = jnp.where(low, pltpu.roll(x, 2 * HD - half, 1), pltpu.roll(x, half, 1))
        return (x * cosine + swapped * sine).astype(jnp.bfloat16)

    loads[0].wait()
    loads[1].wait()
    for i in range(KVH // 2):
        kv_own[:, i * 2 * HD:(i + 1) * 2 * HD] = rotated(k_raw[:, i * 2 * HD:(i + 1) * 2 * HD])
    kv_own[:, KVH * HD:] = v_raw[...]

    def peer_of(side, dz, cc, sign=1):
        zz = lax.rem(z + dz, z_count) if sign > 0 else lax.rem(z + z_count - dz, z_count)
        return (zz * 2 + (1 - y if side else y)) * 2 + (1 - c if cc else c)

    relative = [(side, dz, cc) for side in range(2) for dz in range(z_count) for cc in range(2)]
    peers = [{"seq": peer_of(*r)} for r in relative[1:]]
    peers += [{"fsdp": lax.rem(f_me + d, fsdp_count)} for d in range(1, fsdp_count)]
    greet(peers)

    kv = gather_plan(kv_own, kv_all, (kzs, kzr, kys, kyr, kcs, kcr, own_sems.at[0]), z_count, z, y, c)
    w = gather_plan(w_own, w_all, (wzs, wzr, wys, wyr, wcs, wcr, own_sems.at[1]), z_count, z, y, c)
    kv[0]()
    kv[1](0)
    loads[2].wait()
    w[0]()
    loads[3].wait()
    for i in range(HEADS // 2):
        pair = rotated(q_raw[:, i * 2 * HD:(i + 1) * 2 * HD]) * jnp.bfloat16(HD ** -0.5)
        g, inside = (2 * i) // group_size, (2 * i) % group_size
        q_rot[g, inside * rows:(inside + 1) * rows, :] = pair[:, :HD]
        q_rot[g, (inside + 1) * rows:(inside + 2) * rows, :] = pair[:, HD:]
    key_row = lax.broadcasted_iota(jnp.int32, (1, key_count), 1)
    span_of_key = jnp.zeros((1, key_count), jnp.int32)
    for i in range(span_ref.shape[1]):
        span_of_key = jnp.where(key_row // HALF == i, span_ref[0, i], span_of_key)
    key_at = span_of_key * HALF + key_row % HALF
    query_at = spot(lax.broadcasted_iota(jnp.int32, (rows, 1), 0))
    bias[...] = jnp.where(key_at <= query_at, 0.0, masked_score)

    chosen = routing_ref[...]
    expert_lane = lax.broadcasted_iota(jnp.int32, (rows, EXPERTS), 1)
    picks = [chosen[:, j:j + 1] == expert_lane for j in range(TOPK)]
    named = sum(p.astype(jnp.float32) for p in picks)
    earlier = lax.broadcasted_iota(jnp.int32, (rows, rows), 1) < lax.broadcasted_iota(
        jnp.int32, (rows, rows), 0
    )
    before = jnp.dot(earlier.astype(jnp.float32), named, preferred_element_type=jnp.float32)
    slots = [
        jnp.sum(jnp.where(p, before, 0.0), axis=1, keepdims=True).astype(jnp.int32) for p in picks
    ]

    for d in range(1, z_count):
        kv[1](d)
    for d in range(z_count):
        kv[2](d)
    w[1](0)
    for load in loads[6:]:
        load.start()
    kv[3]()

    chunk = 4

    def send_rows(g):
        return [
            remote(
                rows_all.at[g, f_me], rows_all.at[g, f_me], as_.at[g, d], ar.at[g, d],
                fsdp=lax.rem(f_me + d, fsdp_count),
            )
            for d in range(1, fsdp_count)
        ]

    row_copies = [send_rows(g) for g in range(KVH)]
    relayed = 1
    for g in range(KVH):
        keys = kv_all[:, :, g * HD:(g + 1) * HD].reshape(key_count, HD)
        vals = kv_all[:, :, (KVH + g) * HD:(KVH + g + 1) * HD].reshape(key_count, HD)
        parts = []
        for part in range(group_size // chunk):
            q = q_rot[g, part * chunk * rows:(part + 1) * chunk * rows, :]
            s = lax.dot_general(q, keys, (((1,), (1,)), ((), ())), preferred_element_type=jnp.float32)
            weights, totals = [], []
            for i in range(chunk):
                sink = sink_ref[0, g * group_size + part * chunk + i]
                one = s[i * rows:(i + 1) * rows, :] + bias[...]
                top = jnp.maximum(jnp.max(one, axis=1, keepdims=True), sink)
                p = jnp.exp(one - top)
                totals.append(jnp.sum(p, axis=1, keepdims=True) + jnp.exp(sink - top))
                weights.append(p.astype(jnp.bfloat16))
            o = jnp.dot(jnp.concatenate(weights, axis=0), vals, preferred_element_type=jnp.float32)
            for i in range(chunk):
                parts.append((o[i * rows:(i + 1) * rows, :] / totals[i]).astype(jnp.bfloat16))
            if part == 0 and g > 0:
                for copy in row_copies[g - 1]:
                    copy.start()
        rows_all[g, pl.ds(f_me, 1)] = jnp.concatenate(parts, axis=1)[None]
        while relayed < z_count and relayed * KVH <= (g + 1) * z_count - KVH:
            w[1](relayed)
            relayed += 1
    for d in range(relayed, z_count):
        w[1](d)
    for copy in row_copies[KVH - 1]:
        copy.start()
    for d in range(z_count):
        w[2](d)
    loads[4].wait()
    loads[5].wait()
    w[3]()

    width = group_size * HD
    count = width // w_own.shape[0]
    total = None
    for g in range(KVH):
        for copy in row_copies[g]:
            copy.wait_recv()
        block = w_all[g * count:(g + 1) * count].reshape(width, w_own.shape[1])
        term = jnp.dot(
            rows_all[g].reshape(fsdp_count * rows, width), block, preferred_element_type=jnp.float32
        )
        total = term if total is None else total + term
    proj[...] = total.astype(jnp.bfloat16).reshape(proj.shape)
    backs = []
    for d in range(1, fsdp_count):
        peer = lax.rem(f_me + d, fsdp_count)
        backs.append(remote(proj.at[peer], got.at[f_me], ps.at[d], pr.at[d], fsdp=peer))
    for copy in backs:
        copy.start()
    got[pl.ds(f_me, 1)] = proj[pl.ds(f_me, 1)]
    kv[4]()
    w[4]()
    for g in range(KVH):
        for copy in row_copies[g]:
            copy.wait_send()
    for copy in backs:
        copy.wait_recv()
    columns = w_own.shape[1]
    for f in range(fsdp_count):
        attended_ref[:, f * columns:(f + 1) * columns] = got[f]
    for copy in backs:
        copy.wait_send()

    stream = res[...].astype(jnp.float32) + attended_ref[...].astype(jnp.float32)
    normed = (
        stream
        * lax.rsqrt(jnp.mean(stream * stream, axis=-1, keepdims=True) + norm_eps)
        * gain_ref[...].astype(jnp.float32)
    ).astype(jnp.bfloat16)
    place_lane = lax.broadcasted_iota(jnp.int32, (rows, EXPERTS * CAP), 1)
    dispatch = sum(
        (place_lane == chosen[:, j:j + 1] * CAP + slots[j]).astype(jnp.float32) for j in range(TOPK)
    ).astype(jnp.bfloat16)
    buffer = lax.dot_general(
        dispatch, normed, (((0,), (0,)), ((), ())), preferred_element_type=jnp.float32
    ).astype(jnp.bfloat16)
    for e in range(EXPERTS):
        x_out[e] = buffer[e * CAP:(e + 1) * CAP, :]

    sends, returns = {}, {}
    for r, rel in enumerate(relative[1:], 1):
        to, source = peer_of(*rel), peer_of(*rel, sign=-1)
        sends[r] = remote(x_out.at[to // copies], arrived.at[r], xs.at[r], xr.at[r], seq=to)
        returns[r] = remote(back.at[r], returned.at[me], bs.at[r], br.at[r], seq=source)
    own = pltpu.make_async_copy(x_out.at[me // copies], arrived.at[0], own_sems.at[2])
    keep = pltpu.make_async_copy(back.at[0], returned.at[me], own_sems.at[3])
    for copy in sends.values():
        copy.start()
    own.start()

    logits = jnp.dot(normed, router[...], preferred_element_type=jnp.float32)
    told = [jnp.sum(jnp.where(p, logits, 0.0), axis=1, keepdims=True) for p in picks]
    gates = [1.0 / sum(jnp.exp(t - told[j]) for t in told) for j in range(TOPK)]
    slot_lane = lax.broadcasted_iota(jnp.int32, (rows, seq_count * CAP), 1)
    mixing = sum(
        jnp.where(
            (slot_lane // (CAP * copies) == chosen[:, j:j + 1]) & (slot_lane % CAP == slots[j]),
            gates[j],
            0.0,
        )
        for j in range(TOPK)
    )
    coarse = mixing.astype(jnp.bfloat16)
    fine = (mixing - coarse.astype(jnp.float32)).astype(jnp.bfloat16)

    for load in loads[6:]:
        load.wait()
    per_side = len(relative) // 2
    for side in range(2):
        for i in range(per_side):
            r = side * per_side + i
            sends[r].wait_recv() if r > 0 else own.wait()
            stacked[i * CAP:(i + 1) * CAP, :] = arrived[r]
        x = stacked[...]
        g = jnp.dot(x, gate[...], preferred_element_type=jnp.float32)
        u = jnp.dot(x, up[...], preferred_element_type=jnp.float32)
        hidden = (g * jax.nn.sigmoid(1.702 * g) * (u + 1.0)).astype(jnp.bfloat16)
        part = jnp.dot(hidden, down[...], preferred_element_type=jnp.float32).astype(jnp.bfloat16)
        for i in range(per_side):
            back[side * per_side + i] = part[i * CAP:(i + 1) * CAP, :]
        for i in range(per_side):
            r = side * per_side + i
            returns[r].start() if r > 0 else keep.start()
    for copy in sends.values():
        copy.wait_send()
    for copy in returns.values():
        copy.wait_recv()
    keep.wait()
    for i in range(seq_count):
        restacked[i * CAP:(i + 1) * CAP, :] = returned[i]
    outs = restacked[...]
    mixed = jnp.dot(coarse, outs, preferred_element_type=jnp.float32) + jnp.dot(
        fine, outs, preferred_element_type=jnp.float32
    )
    layer_ref[...] = (
        res[...].astype(jnp.float32) + attended_ref[...].astype(jnp.float32) + mixed
    ).astype(jnp.bfloat16)
    for copy in returns.values():
        copy.wait_send()


def on_device(
    residual,
    queries,
    key_rows,
    values,
    attention_sinks,
    out_weight,
    norm_gain,
    router_weight,
    gate_weight,
    up_weight,
    down_weight,
    routing,
    span_order,
):
    seq_count = lax.axis_size("seq")
    fsdp_count = lax.axis_size("fsdp")
    z_count = seq_count // 4
    rows = residual.shape[1]
    dma = pltpu.SemaphoreType.DMA
    vmem = pl.BlockSpec(memory_space=pltpu.VMEM)
    smem = pl.BlockSpec(memory_space=pltpu.SMEM)
    hbm = pl.BlockSpec(memory_space=pl.ANY)
    gather_sems = [dma((z_count,))] * 4 + [dma((2, z_count))] * 2

    def held(*shape):
        return pltpu.VMEM(shape, jnp.bfloat16)

    kv_width = 2 * KVH * HD
    w_rows, columns = out_weight.shape
    attended, layer_output = pl.pallas_call(
        functools.partial(layer_kernel, seq_count, fsdp_count),
        out_shape=[jax.ShapeDtypeStruct((rows, D), jnp.bfloat16)] * 2,
        in_specs=[smem, smem, vmem, vmem] + [hbm] * 9,
        out_specs=[vmem, vmem],
        scratch_shapes=[
            held(rows, D),
            held(rows, HEADS * HD),
            held(rows, KVH * HD),
            held(rows, KVH * HD),
            held(*router_weight.shape),
            held(*gate_weight.shape),
            held(*up_weight.shape),
            held(*down_weight.shape),
            held(rows, kv_width),
            held(seq_count, rows, kv_width),
            held(w_rows, columns),
            held(seq_count, w_rows, columns),
            held(KVH, HEADS // KVH * rows, HD),
            pltpu.VMEM((rows, seq_count * rows), jnp.float32),
            held(KVH, fsdp_count, rows, HEADS // KVH * HD),
            held(fsdp_count, rows, columns),
            held(fsdp_count, rows, columns),
            held(EXPERTS, CAP, D),
            held(seq_count, CAP, D),
            held(seq_count // 2 * CAP, D),
            held(seq_count, CAP, D),
            held(seq_count, CAP, D),
            held(seq_count * CAP, D),
            dma((9,)),
        ]
        + gather_sems
        + gather_sems
        + [dma((4,)), dma((KVH, fsdp_count)), dma((KVH, fsdp_count)), dma((fsdp_count,)), dma((fsdp_count,))]
        + [dma((seq_count,))] * 4,
        compiler_params=pltpu.CompilerParams(
            collective_id=0, has_side_effects=True, vmem_limit_bytes=60 * 1024 * 1024
        ),
    )(
        attention_sinks[None, :],
        span_order[None, :],
        norm_gain[None, :],
        routing[0],
        residual[0],
        queries[0],
        key_rows[0],
        values[0],
        out_weight,
        router_weight,
        gate_weight,
        up_weight,
        down_weight,
    )
    return (attended[None], layer_output[None])


def solution(mesh):
    in_specs = (
        P("fsdp", "seq", None),
        P("fsdp", "seq", None),
        P("fsdp", "seq", None),
        P("fsdp", "seq", None),
        P(),
        P("seq", "fsdp"),
        P(),
        P(),
        P(None, "seq"),
        P(None, "seq"),
        P("seq", None),
        P("fsdp", "seq", None),
        P(),
    )
    out_specs = (P("fsdp", "seq", None), P("fsdp", "seq", None))
    return jax.shard_map(
        on_device, mesh=mesh, in_specs=in_specs, out_specs=out_specs, check_vma=False
    )
```

profile of v0, /device:TPU:0, one launch (start us, length us, event | category | flops | bytes accessed | tf_op | source)
XLA Modules:
  0.0 104.0 jit_solution(1987266019710095796)
XLA Ops:
  0.6 1.3 %broadcast_in_dim.17.gain_ref = bf16[1,1440]{1,0:T(2,128)(2,1)} reshape(bf16[1440]{0:T(1024)(128)(2,1)} %param.19) | data formatting | bytes 5760 | tf_op jit(solution)/shard_map/broadcast_in_dim | solution.py:433
  1.9 1.4 %copy.15.routing_ref = s32[64,2]{1,0:T(8,128)} copy(s32[64,2]{0,1:T(2,128)} %bitcast.15) | data formatting | bytes 1024 | tf_op jit(solution)/shard_map/squeeze | solution.py:434
  3.3 1.7 %copy.16.w_hbm = bf16[128,720]{1,0:T(8,128)(2,1)} copy(bf16[128,720]{0,1:T(8,128)(2,1)} %param.18) | data formatting | bytes 368640 | tf_op args[5]
  5.0 1.7 %copy.17.router_hbm = bf16[1440,16]{1,0:T(8,128)(2,1)} copy(bf16[1440,16]{0,1:T(8,128)(2,1)} %param.20) | data formatting | bytes 92160 | tf_op args[7]
  6.7 94.0 %shard_map.140 = (bf16[64,1440]{1,0:T(8,128)(2,1)}, bf16[64,1440]{1,0:T(8,128)(2,1)}) custom-call(f32[1,32]{1,0:T(1,128)} %bitcast.16, s32[1,32]{1,0:T(1,128)} %bitcast.17, bf16[1,1440]{1,0:T(2,128)(2,1)} %broadcast_in_dim.17.gain_ref, s32[64,2]{1,0:T(8,128)} %copy.15.routing_ref, bf16[64,1440]{1,0:T(8,128)(2,1)} %bitcast.10, bf16[64,2048]{1,0:T(8,128)(2,1)} %bitcast.9, ...), custom_call_target="tpu_custom_call" | custom-call | tf_op jit(solution)/shard_map/pallas_call | solution.py:392
  100.7 1.6 %copy.20 = bf16[1,64,1440]{2,1,0:T(8,128)(2,1)} copy(bf16[1,64,1440]{2,1,0:T(8,128)(2,1)} %bitcast.12) | data formatting | bytes 368640
  102.4 1.6 %copy.21 = bf16[1,64,1440]{2,1,0:T(8,128)(2,1)} copy(bf16[1,64,1440]{2,1,0:T(8,128)(2,1)} %bitcast.11) | data formatting | bytes 368640
where the time goes:
time: 104 us
  Pallas kernels  94 us (90%)
  local copies, waits for them, and re-layouts  9.34 us (9%)
    pallas_call x1, Pallas kernels, on_device(): pl.pallas_call(functools.partial(layer_kernel, seq_count, fsdp_count), ou...  94 us
    unnamed x4, local copies, waits for them, and re-layouts  6.68 us

commit v1 on v0

--- a/solution.py
+++ b/solution.py
@@ -104,7 +104,7 @@
     seq_count, fsdp_count,
     sink_ref, span_ref, gain_ref, routing_ref,
     res_hbm, q_hbm, k_hbm, v_hbm, w_hbm, router_hbm, gate_hbm, up_hbm, down_hbm,
-    attended_ref, layer_ref,
+    out_ref,
     res, q_raw, k_raw, v_raw, router, gate, up, down,
     kv_own, kv_all, w_own, w_all, q_rot, bias, rows_all, proj, got,
     x_out, arrived, stacked, back, returned, restacked,
@@ -181,15 +181,15 @@
     bias[...] = jnp.where(key_at <= query_at, 0.0, masked_score)
 
     chosen = routing_ref[...]
-    expert_lane = lax.broadcasted_iota(jnp.int32, (rows, EXPERTS), 1)
-    picks = [chosen[:, j:j + 1] == expert_lane for j in range(TOPK)]
+    expert_row = lax.broadcasted_iota(jnp.int32, (EXPERTS, rows), 0)
+    picks = [chosen[j:j + 1, :] == expert_row for j in range(TOPK)]
     named = sum(p.astype(jnp.float32) for p in picks)
-    earlier = lax.broadcasted_iota(jnp.int32, (rows, rows), 1) < lax.broadcasted_iota(
-        jnp.int32, (rows, rows), 0
-    )
-    before = jnp.dot(earlier.astype(jnp.float32), named, preferred_element_type=jnp.float32)
+    earlier = lax.broadcasted_iota(jnp.int32, (rows, rows), 0) < lax.broadcasted_iota(
+        jnp.int32, (rows, rows), 1
+    )
+    before = jnp.dot(named, earlier.astype(jnp.float32), preferred_element_type=jnp.float32)
     slots = [
-        jnp.sum(jnp.where(p, before, 0.0), axis=1, keepdims=True).astype(jnp.int32) for p in picks
+        jnp.sum(jnp.where(p, before, 0.0), axis=0, keepdims=True).astype(jnp.int32) for p in picks
     ]
 
     for d in range(1, z_count):
@@ -250,16 +250,22 @@
     w[3]()
 
     width = group_size * HD
-    count = width // w_own.shape[0]
+    w_rows = w_own.shape[1]
+    count = width // w_rows
+    pair = max(1, 256 // w_rows)
     total = None
     for g in range(KVH):
         for copy in row_copies[g]:
             copy.wait_recv()
-        block = w_all[g * count:(g + 1) * count].reshape(width, w_own.shape[1])
-        term = jnp.dot(
-            rows_all[g].reshape(fsdp_count * rows, width), block, preferred_element_type=jnp.float32
-        )
-        total = term if total is None else total + term
+        for first in range(0, count, pair):
+            block = jnp.concatenate([w_all[g * count + first + i] for i in range(pair)], axis=1)
+            term = lax.dot_general(
+                rows_all[g, :, :, first * w_rows:(first + pair) * w_rows].reshape(
+                    fsdp_count * rows, pair * w_rows
+                ),
+                block, (((1,), (1,)), ((), ())), preferred_element_type=jnp.float32,
+            )
+            total = term if total is None else total + term
     proj[...] = total.astype(jnp.bfloat16).reshape(proj.shape)
     backs = []
     for d in range(1, fsdp_count):
@@ -275,25 +281,23 @@
             copy.wait_send()
     for copy in backs:
         copy.wait_recv()
-    columns = w_own.shape[1]
+    columns = w_own.shape[0]
     for f in range(fsdp_count):
-        attended_ref[:, f * columns:(f + 1) * columns] = got[f]
+        out_ref[0, :, f * columns:(f + 1) * columns] = got[f]
     for copy in backs:
         copy.wait_send()
 
-    stream = res[...].astype(jnp.float32) + attended_ref[...].astype(jnp.float32)
+    stream = res[...].astype(jnp.float32) + out_ref[0].astype(jnp.float32)
     normed = (
         stream
         * lax.rsqrt(jnp.mean(stream * stream, axis=-1, keepdims=True) + norm_eps)
-        * gain_ref[...].astype(jnp.float32)
+        * gain_ref[...][None, :].astype(jnp.float32)
     ).astype(jnp.bfloat16)
-    place_lane = lax.broadcasted_iota(jnp.int32, (rows, EXPERTS * CAP), 1)
+    place = lax.broadcasted_iota(jnp.int32, (EXPERTS * CAP, rows), 0)
     dispatch = sum(
-        (place_lane == chosen[:, j:j + 1] * CAP + slots[j]).astype(jnp.float32) for j in range(TOPK)
+        (place == chosen[j:j + 1, :] * CAP + slots[j]).astype(jnp.float32) for j in range(TOPK)
     ).astype(jnp.bfloat16)
-    buffer = lax.dot_general(
-        dispatch, normed, (((0,), (0,)), ((), ())), preferred_element_type=jnp.float32
-    ).astype(jnp.bfloat16)
+    buffer = jnp.dot(dispatch, normed, preferred_element_type=jnp.float32).astype(jnp.bfloat16)
     for e in range(EXPERTS):
         x_out[e] = buffer[e * CAP:(e + 1) * CAP, :]
 
@@ -308,13 +312,15 @@
         copy.start()
     own.start()
 
-    logits = jnp.dot(normed, router[...], preferred_element_type=jnp.float32)
-    told = [jnp.sum(jnp.where(p, logits, 0.0), axis=1, keepdims=True) for p in picks]
+    logits = lax.dot_general(
+        router[...], normed, (((1,), (1,)), ((), ())), preferred_element_type=jnp.float32
+    )
+    told = [jnp.sum(jnp.where(p, logits, 0.0), axis=0, keepdims=True) for p in picks]
     gates = [1.0 / sum(jnp.exp(t - told[j]) for t in told) for j in range(TOPK)]
-    slot_lane = lax.broadcasted_iota(jnp.int32, (rows, seq_count * CAP), 1)
+    slot_row = lax.broadcasted_iota(jnp.int32, (seq_count * CAP, rows), 0)
     mixing = sum(
         jnp.where(
-            (slot_lane // (CAP * copies) == chosen[:, j:j + 1]) & (slot_lane % CAP == slots[j]),
+            (slot_row // (CAP * copies) == chosen[j:j + 1, :]) & (slot_row % CAP == slots[j]),
             gates[j],
             0.0,
         )
@@ -349,12 +355,11 @@
     for i in range(seq_count):
         restacked[i * CAP:(i + 1) * CAP, :] = returned[i]
     outs = restacked[...]
-    mixed = jnp.dot(coarse, outs, preferred_element_type=jnp.float32) + jnp.dot(
-        fine, outs, preferred_element_type=jnp.float32
-    )
-    layer_ref[...] = (
-        res[...].astype(jnp.float32) + attended_ref[...].astype(jnp.float32) + mixed
-    ).astype(jnp.bfloat16)
+    by_slot = (((0,), (0,)), ((), ()))
+    mixed = lax.dot_general(coarse, outs, by_slot, preferred_element_type=jnp.float32) + lax.dot_general(
+        fine, outs, by_slot, preferred_element_type=jnp.float32
+    )
+    out_ref[1] = (res[...].astype(jnp.float32) + out_ref[0].astype(jnp.float32) + mixed).astype(jnp.bfloat16)
     for copy in returns.values():
         copy.wait_send()
 
@@ -389,24 +394,24 @@
 
     kv_width = 2 * KVH * HD
     w_rows, columns = out_weight.shape
-    attended, layer_output = pl.pallas_call(
+    both = pl.pallas_call(
         functools.partial(layer_kernel, seq_count, fsdp_count),
-        out_shape=[jax.ShapeDtypeStruct((rows, D), jnp.bfloat16)] * 2,
+        out_shape=jax.ShapeDtypeStruct((2, rows, D), jnp.bfloat16),
         in_specs=[smem, smem, vmem, vmem] + [hbm] * 9,
-        out_specs=[vmem, vmem],
+        out_specs=vmem,
         scratch_shapes=[
             held(rows, D),
             held(rows, HEADS * HD),
             held(rows, KVH * HD),
             held(rows, KVH * HD),
-            held(*router_weight.shape),
+            held(*router_weight.shape[::-1]),
             held(*gate_weight.shape),
             held(*up_weight.shape),
             held(*down_weight.shape),
             held(rows, kv_width),
             held(seq_count, rows, kv_width),
-            held(w_rows, columns),
-            held(seq_count, w_rows, columns),
+            held(columns, w_rows),
+            held(seq_count, columns, w_rows),
             held(KVH, HEADS // KVH * rows, HD),
             pltpu.VMEM((rows, seq_count * rows), jnp.float32),
             held(KVH, fsdp_count, rows, HEADS // KVH * HD),
@@ -430,19 +435,19 @@
     )(
         attention_sinks[None, :],
         span_order[None, :],
-        norm_gain[None, :],
-        routing[0],
+        norm_gain,
+        routing[0].T,
         residual[0],
         queries[0],
         key_rows[0],
         values[0],
-        out_weight,
-        router_weight,
+        out_weight.T,
+        router_weight.T,
         gate_weight,
         up_weight,
         down_weight,
     )
-    return (attended[None], layer_output[None])
+    return (both[0][None], both[1][None])
 
 
 def solution(mesh):

time: 104 us -> 95.9 us (0.922)
  local copies, waits for them, and re-layouts: 9.34 us -> 1.79 us
    unnamed x4 -> x0, local copies, waits for them, and re-layouts: 6.68 us -> none
    slice x0 -> x1, local copies, waits for them, and re-layouts: none -> 1.79 us  [on_device(): return (both[0][None], both[1][None])]
    squeeze x1 -> x0, local copies, waits for them, and re-layouts: 1.38 us -> none  [on_device(): routing[0]]
    broadcast_in_dim x1 -> x0, local copies, waits for them, and re-layouts: 1.28 us -> none  [on_device(): norm_gain[None, :]]
where the time goes in v1:
time: 95.9 us; the launch traced here: 95.8 us
  Pallas kernels  93.3 us (97%)
  local copies, waits for them, and re-layouts  1.79 us (2%)
    pallas_call x1, Pallas kernels, on_device(): pl.pallas_call(functools.partial(layer_kernel, seq_count, fsdp_count), ou...  93.3 us

profile of v1, /device:TPU:0, one launch (start us, length us, event | category | flops | bytes accessed | tf_op | source)
XLA Modules:
  0.0 95.8 jit_solution(17779379123543244212)
XLA Ops:
  0.6 93.3 %shard_map.140 = bf16[2,64,1440]{2,1,0:T(8,128)(2,1)} custom-call(f32[1,32]{1,0:T(1,128)} %bitcast.18, s32[1,32]{1,0:T(1,128)} %bitcast.19, bf16[1440]{0:T(1024)(128)(2,1)} %gain_ref.1, s32[2,64]{1,0:T(2,128)} %bitcast.17, bf16[64,1440]{1,0:T(8,128)(2,1)} %bitcast.12, bf16[64,2048]{1,0:T(8,128)(2,1)} %bitcast.11, bf16[64,256]{1,0:T(8,128)(2,1)} %bitcast.15, ...), custom_call_target="tpu_custom_call" | custom-call | tf_op jit(solution)/shard_map/pallas_call | solution.py:397
  94.0 1.8 %fusion = (bf16[1,64,1440]{2,1,0:T(8,128)(2,1)}, bf16[1,64,1440]{2,1,0:T(8,128)(2,1)}) fusion(bf16[2,64,1440]{2,1,0:T(8,128)(2,1)} %shard_map.140), kind=kLoop, calls=%fused_computation | loop fusion | bytes 737280 | tf_op jit(solution)/shard_map/slice | solution.py:450

commit v2 on v1

--- a/solution.py
+++ b/solution.py
@@ -44,36 +44,34 @@
     pl.semaphore_wait(barrier, len(peers))
 
 
-def gather_plan(block, slots, sems, z_count, z, y, c):
-    z_send, z_recv, y_send, y_recv, c_send, c_recv, own_sem = sems
-
-    def slot(zz, yy, cc):
-        return (zz * 2 + yy) * 2 + cc
+def slot(z, y, c):
+    return (z * 2 + y) * 2 + c
+
+
+def gather_plan(slots, sems, z_count, z, y, c):
+    z_send, z_recv, y_send, y_recv, c_send, c_recv = sems
 
     def z_of(d):
         return lax.rem(z + z_count - d, z_count)
 
-    own = slot(z, y, c)
+    own = slots.at[slot(z, y, c)]
     to_z = [
-        remote(block, slots.at[own], z_send.at[d], z_recv.at[d], seq=slot(lax.rem(z + d, z_count), y, c))
+        remote(own, own, z_send.at[d], z_recv.at[d], seq=slot(lax.rem(z + d, z_count), y, c))
         for d in range(1, z_count)
     ]
 
     def to_y(d):
-        source = block if d == 0 else slots.at[slot(z_of(d), y, c)]
-        return remote(source, slots.at[slot(z_of(d), y, c)], y_send.at[d], y_recv.at[d], seq=slot(z, 1 - y, c))
+        block = slots.at[slot(z_of(d), y, c)]
+        return remote(block, block, y_send.at[d], y_recv.at[d], seq=slot(z, 1 - y, c))
 
     def to_c(side, d):
-        index = slot(z_of(d), y if side == 0 else 1 - y, c)
-        source = block if side == 0 and d == 0 else slots.at[index]
-        return remote(source, slots.at[index], c_send.at[side, d], c_recv.at[side, d], seq=slot(z, y, 1 - c))
-
-    local = pltpu.make_async_copy(block, slots.at[own], own_sem)
+        block = slots.at[slot(z_of(d), y if side == 0 else 1 - y, c)]
+        return remote(block, block, c_send.at[side, d], c_recv.at[side, d], seq=slot(z, y, 1 - c))
+
     ys = [to_y(d) for d in range(z_count)]
     cs = [[to_c(side, d) for d in range(z_count)] for side in range(2)]
 
     def start_z():
-        local.start()
         for copy in to_z:
             copy.start()
 
@@ -91,13 +89,93 @@
         for side in range(2):
             for d in range(z_count):
                 cs[side][d].wait_recv()
-        local.wait()
 
     def drain():
         for copy in to_z + ys + cs[0] + cs[1]:
             copy.wait_send()
 
     return start_z, relay, relay_across, finish, drain
+
+
+def line_plan(slots, pieces, sems, z_count, z, y, c):
+    z_send, z_recv, y_send, y_recv, c_send, c_recv = sems
+    last = z_count - 1
+
+    def block(zz, yy, p):
+        return slots.at[slot(zz, yy, c), pl.ds(*pieces[p])]
+
+    def along(way, zz, p):
+        part = block(zz, y, p)
+        return remote(part, part, z_send.at[way, zz, p], z_recv.at[zz, p], seq=slot(z + 1 - 2 * way, y, c))
+
+    def over(zz, p):
+        part = block(zz, y, p)
+        return remote(part, part, y_send.at[zz, p], y_recv.at[zz, p], seq=slot(z, 1 - y, c))
+
+    def beside(side, zz, p):
+        part = block(zz, 1 - y if side else y, p)
+        return remote(part, part, c_send.at[side, zz, p], c_recv.at[side, zz, p], seq=slot(z, y, 1 - c))
+
+    def onward(way, zz, p):
+        @pl.when(z < last if way == 0 else z > 0)
+        def _():
+            along(way, zz, p).start()
+
+    def start(p):
+        onward(0, z, p)
+        onward(1, z, p)
+        over(z, p).start()
+        beside(0, z, p).start()
+
+    def each(k, act):
+        for way in range(2):
+            zz = z - 1 - k if way == 0 else z + 1 + k
+
+            @pl.when(zz >= 0 if way == 0 else zz <= last)
+            def _(way=way, zz=zz):
+                act(way, zz)
+
+    def relay(k, p):
+        def act(way, zz):
+            along(way, zz, p).wait_recv()
+            onward(way, zz, p)
+            over(zz, p).start()
+            beside(0, zz, p).start()
+
+        each(k, act)
+
+    def across(k, p):
+        def act(way, zz):
+            over(zz, p).wait_recv()
+            beside(1, zz, p).start()
+
+        if k < 0:
+            act(0, z)
+        else:
+            each(k, act)
+
+    every = [(zz, p) for zz in range(z_count) for p in range(len(pieces))]
+
+    def finish():
+        for zz, p in every:
+            for side in range(2):
+                beside(side, zz, p).wait_recv()
+
+    def drain():
+        for zz, p in every:
+            @pl.when((z >= zz) & (z < last))
+            def _():
+                along(0, zz, p).wait_send()
+
+            @pl.when((z <= zz) & (z > 0))
+            def _():
+                along(1, zz, p).wait_send()
+
+            over(zz, p).wait_send()
+            for side in range(2):
+                beside(side, zz, p).wait_send()
+
+    return start, relay, across, finish, drain
 
 
 def layer_kernel(
@@ -106,22 +184,22 @@
     res_hbm, q_hbm, k_hbm, v_hbm, w_hbm, router_hbm, gate_hbm, up_hbm, down_hbm,
     out_ref,
     res, q_raw, k_raw, v_raw, router, gate, up, down,
-    kv_own, kv_all, w_own, w_all, q_rot, bias, rows_all, proj, got,
-    x_out, arrived, stacked, back, returned, restacked,
+    kv_all, w_all, q_rot, bias, rows_all, proj, got,
+    x_out, arrived, stacked, back, returned, mix,
     load_sems,
     kzs, kzr, kys, kyr, kcs, kcr, wzs, wzr, wys, wyr, wcs, wcr, own_sems, as_, ar, ps, pr,
     xs, xr, bs, br,
 ):
+    me = lax.axis_index("seq")
+    f_me = lax.axis_index("fsdp")
     sources = (k_hbm, v_hbm, w_hbm, q_hbm, res_hbm, router_hbm, gate_hbm, up_hbm, down_hbm)
-    targets = (k_raw, v_raw, w_own, q_raw, res, router, gate, up, down)
+    targets = (k_raw, v_raw, w_all.at[me], q_raw, res, router, gate, up, down)
     loads = [
         pltpu.make_async_copy(a, b, load_sems.at[i]) for i, (a, b) in enumerate(zip(sources, targets))
     ]
     for load in loads[:6]:
         load.start()
 
-    me = lax.axis_index("seq")
-    f_me = lax.axis_index("fsdp")
     z_count = seq_count // 4
     z, y, c = me // 4, lax.rem(me // 2, 2), lax.rem(me, 2)
     rows, key_count = bias.shape
@@ -147,25 +225,34 @@
 
     loads[0].wait()
     loads[1].wait()
-    for i in range(KVH // 2):
-        kv_own[:, i * 2 * HD:(i + 1) * 2 * HD] = rotated(k_raw[:, i * 2 * HD:(i + 1) * 2 * HD])
-    kv_own[:, KVH * HD:] = v_raw[...]
-
-    def peer_of(side, dz, cc, sign=1):
-        zz = lax.rem(z + dz, z_count) if sign > 0 else lax.rem(z + z_count - dz, z_count)
+    keys = [rotated(k_raw[:, i * 2 * HD:(i + 1) * 2 * HD]) for i in range(KVH // 2)]
+    kv_all[pl.ds(me, 1)] = jnp.concatenate(keys + [v_raw[...]], axis=1)[None]
+
+    reach = z_count // 2
+    base, inner = z // reach, lax.rem(z, reach)
+
+    def peer_of(far, j, side, cc, sign=1):
+        step = lax.rem(inner + j, reach) if sign > 0 else lax.rem(inner + reach - j, reach)
+        zz = (1 - base if far else base) * reach + step
         return (zz * 2 + (1 - y if side else y)) * 2 + (1 - c if cc else c)
 
-    relative = [(side, dz, cc) for side in range(2) for dz in range(z_count) for cc in range(2)]
+    relative = [
+        (far, j, side, cc) for far in range(2) for j in range(reach) for side in range(2) for cc in range(2)
+    ]
     peers = [{"seq": peer_of(*r)} for r in relative[1:]]
     peers += [{"fsdp": lax.rem(f_me + d, fsdp_count)} for d in range(1, fsdp_count)]
     greet(peers)
 
-    kv = gather_plan(kv_own, kv_all, (kzs, kzr, kys, kyr, kcs, kcr, own_sems.at[0]), z_count, z, y, c)
-    w = gather_plan(w_own, w_all, (wzs, wzr, wys, wyr, wcs, wcr, own_sems.at[1]), z_count, z, y, c)
+    w_columns, w_rows = w_all.shape[1:]
+    cut = w_columns // 32 * 16
+    pieces = [(0, cut), (cut, w_columns - cut)] if w_columns % 16 == 0 else [(0, w_columns)]
+    kv = gather_plan(kv_all, (kzs, kzr, kys, kyr, kcs, kcr), z_count, z, y, c)
+    w = line_plan(w_all, pieces, (wzs, wzr, wys, wyr, wcs, wcr), z_count, z, y, c)
     kv[0]()
     kv[1](0)
     loads[2].wait()
-    w[0]()
+    for p in range(len(pieces)):
+        w[0](p)
     loads[3].wait()
     for i in range(HEADS // 2):
         pair = rotated(q_raw[:, i * 2 * HD:(i + 1) * 2 * HD]) * jnp.bfloat16(HD ** -0.5)
@@ -194,11 +281,20 @@
 
     for d in range(1, z_count):
         kv[1](d)
+    for load in loads[6:]:
+        load.start()
+    steps = [functools.partial(w[1], 0, p) for p in range(len(pieces))]
+    steps += [functools.partial(w[2], -1, p) for p in range(len(pieces))]
+    for k in range(1, z_count - 1):
+        for p in range(len(pieces)):
+            steps += [functools.partial(w[1], k, p), functools.partial(w[2], k - 1, p)]
+    closing = [functools.partial(w[2], z_count - 2, p) for p in range(len(pieces))]
+    early = len(pieces)
+    steps.pop(0)()
     for d in range(z_count):
         kv[2](d)
-    w[1](0)
-    for load in loads[6:]:
-        load.start()
+    for _ in range(early - 1):
+        steps.pop(0)()
     kv[3]()
 
     chunk = 4
@@ -213,7 +309,8 @@
         ]
 
     row_copies = [send_rows(g) for g in range(KVH)]
-    relayed = 1
+    turns = KVH * group_size // chunk
+    share = -(-len(steps) // turns)
     for g in range(KVH):
         keys = kv_all[:, :, g * HD:(g + 1) * HD].reshape(key_count, HD)
         vals = kv_all[:, :, (KVH + g) * HD:(KVH + g + 1) * HD].reshape(key_count, HD)
@@ -235,22 +332,19 @@
             if part == 0 and g > 0:
                 for copy in row_copies[g - 1]:
                     copy.start()
+            for step in steps[:share]:
+                step()
+            steps = steps[share:]
         rows_all[g, pl.ds(f_me, 1)] = jnp.concatenate(parts, axis=1)[None]
-        while relayed < z_count and relayed * KVH <= (g + 1) * z_count - KVH:
-            w[1](relayed)
-            relayed += 1
-    for d in range(relayed, z_count):
-        w[1](d)
     for copy in row_copies[KVH - 1]:
         copy.start()
-    for d in range(z_count):
-        w[2](d)
+    for step in steps + closing:
+        step()
     loads[4].wait()
     loads[5].wait()
     w[3]()
 
     width = group_size * HD
-    w_rows = w_own.shape[1]
     count = width // w_rows
     pair = max(1, 256 // w_rows)
     total = None
@@ -281,9 +375,8 @@
             copy.wait_send()
     for copy in backs:
         copy.wait_recv()
-    columns = w_own.shape[0]
     for f in range(fsdp_count):
-        out_ref[0, :, f * columns:(f + 1) * columns] = got[f]
+        out_ref[0, :, f * w_columns:(f + 1) * w_columns] = got[f]
     for copy in backs:
         copy.wait_send()
 
@@ -293,13 +386,27 @@
         * lax.rsqrt(jnp.mean(stream * stream, axis=-1, keepdims=True) + norm_eps)
         * gain_ref[...][None, :].astype(jnp.float32)
     ).astype(jnp.bfloat16)
-    place = lax.broadcasted_iota(jnp.int32, (EXPERTS * CAP, rows), 0)
+    fold = x_out.shape[2]
+    spare = 2 * fold - D
+    column = lax.broadcasted_iota(jnp.int32, (1, 2 * rows), 1)
+    wrap = column // rows
+    chosen_twice = jnp.concatenate([chosen, chosen], axis=1)
+    slot_twice = [jnp.concatenate([slots[j], slots[j]], axis=1) for j in range(TOPK)]
+    place = lax.broadcasted_iota(jnp.int32, (EXPERTS * 2 * CAP, 2 * rows), 0)
     dispatch = sum(
-        (place == chosen[j:j + 1, :] * CAP + slots[j]).astype(jnp.float32) for j in range(TOPK)
+        (place == chosen_twice[j:j + 1, :] * (2 * CAP) + wrap * CAP + slot_twice[j]).astype(jnp.float32)
+        for j in range(TOPK)
     ).astype(jnp.bfloat16)
-    buffer = jnp.dot(dispatch, normed, preferred_element_type=jnp.float32).astype(jnp.bfloat16)
+
+    def folded(wide):
+        right = jnp.concatenate([wide[:, fold:], jnp.zeros((wide.shape[0], spare), wide.dtype)], axis=1)
+        return wide[:, :fold], right
+
+    buffer = jnp.dot(
+        dispatch, jnp.concatenate(folded(normed), axis=0), preferred_element_type=jnp.float32
+    ).astype(jnp.bfloat16)
     for e in range(EXPERTS):
-        x_out[e] = buffer[e * CAP:(e + 1) * CAP, :]
+        x_out[e] = buffer[e * 2 * CAP:(e + 1) * 2 * CAP, :]
 
     sends, returns = {}, {}
     for r, rel in enumerate(relative[1:], 1):
@@ -317,49 +424,53 @@
     )
     told = [jnp.sum(jnp.where(p, logits, 0.0), axis=0, keepdims=True) for p in picks]
     gates = [1.0 / sum(jnp.exp(t - told[j]) for t in told) for j in range(TOPK)]
-    slot_row = lax.broadcasted_iota(jnp.int32, (seq_count * CAP, rows), 0)
+    slot_row = lax.broadcasted_iota(jnp.int32, (seq_count * 2 * CAP, 2 * rows), 0)
+    within = slot_row % (2 * CAP)
     mixing = sum(
         jnp.where(
-            (slot_row // (CAP * copies) == chosen[j:j + 1, :]) & (slot_row % CAP == slots[j]),
-            gates[j],
+            (slot_row // (2 * CAP * copies) == chosen_twice[j:j + 1, :])
+            & (within == wrap * CAP + slot_twice[j]),
+            jnp.concatenate([gates[j], gates[j]], axis=1),
             0.0,
         )
         for j in range(TOPK)
     )
-    coarse = mixing.astype(jnp.bfloat16)
-    fine = (mixing - coarse.astype(jnp.float32)).astype(jnp.bfloat16)
+    coarse = mixing.astype(jnp.bfloat16).astype(jnp.float32)
+    mix[...] = jnp.concatenate([coarse, mixing - coarse], axis=1).T.astype(jnp.bfloat16)
 
     for load in loads[6:]:
         load.wait()
-    per_side = len(relative) // 2
-    for side in range(2):
-        for i in range(per_side):
-            r = side * per_side + i
+    near = len(relative) // 2
+    chunks = [range(near), range(near, near + near // 2), range(near + near // 2, 2 * near)]
+    for chunk in chunks:
+        for i, r in enumerate(chunk):
             sends[r].wait_recv() if r > 0 else own.wait()
-            stacked[i * CAP:(i + 1) * CAP, :] = arrived[r]
-        x = stacked[...]
+            block = arrived[r]
+            stacked[i * CAP:(i + 1) * CAP, :fold] = block[:CAP, :]
+            stacked[i * CAP:(i + 1) * CAP, fold:] = block[CAP:, :D - fold]
+        x = stacked[:len(chunk) * CAP, :]
         g = jnp.dot(x, gate[...], preferred_element_type=jnp.float32)
         u = jnp.dot(x, up[...], preferred_element_type=jnp.float32)
         hidden = (g * jax.nn.sigmoid(1.702 * g) * (u + 1.0)).astype(jnp.bfloat16)
         part = jnp.dot(hidden, down[...], preferred_element_type=jnp.float32).astype(jnp.bfloat16)
-        for i in range(per_side):
-            back[side * per_side + i] = part[i * CAP:(i + 1) * CAP, :]
-        for i in range(per_side):
-            r = side * per_side + i
+        left, right = folded(part)
+        for i, r in enumerate(chunk):
+            back[r, :CAP] = left[i * CAP:(i + 1) * CAP, :]
+            back[r, CAP:] = right[i * CAP:(i + 1) * CAP, :]
+        for r in chunk:
             returns[r].start() if r > 0 else keep.start()
     for copy in sends.values():
         copy.wait_send()
     for copy in returns.values():
         copy.wait_recv()
     keep.wait()
-    for i in range(seq_count):
-        restacked[i * CAP:(i + 1) * CAP, :] = returned[i]
-    outs = restacked[...]
-    by_slot = (((0,), (0,)), ((), ()))
-    mixed = lax.dot_general(coarse, outs, by_slot, preferred_element_type=jnp.float32) + lax.dot_general(
-        fine, outs, by_slot, preferred_element_type=jnp.float32
-    )
-    out_ref[1] = (res[...].astype(jnp.float32) + out_ref[0].astype(jnp.float32) + mixed).astype(jnp.bfloat16)
+    parts = jnp.dot(
+        mix[...], returned[...].reshape(seq_count * 2 * CAP, fold), preferred_element_type=jnp.float32
+    )
+    mixed = [parts[h * rows:(h + 1) * rows, :] + parts[(2 + h) * rows:(3 + h) * rows, :] for h in range(2)]
+    stream = res[...].astype(jnp.float32) + out_ref[0].astype(jnp.float32)
+    out_ref[1, :, :fold] = (stream[:, :fold] + mixed[0]).astype(jnp.bfloat16)
+    out_ref[1, :, fold:] = (stream[:, fold:] + mixed[1][:, :D - fold]).astype(jnp.bfloat16)
     for copy in returns.values():
         copy.wait_send()
 
@@ -387,12 +498,12 @@
     vmem = pl.BlockSpec(memory_space=pltpu.VMEM)
     smem = pl.BlockSpec(memory_space=pltpu.SMEM)
     hbm = pl.BlockSpec(memory_space=pl.ANY)
-    gather_sems = [dma((z_count,))] * 4 + [dma((2, z_count))] * 2
 
     def held(*shape):
         return pltpu.VMEM(shape, jnp.bfloat16)
 
     kv_width = 2 * KVH * HD
+    fold = -(-D // 256) * 128
     w_rows, columns = out_weight.shape
     both = pl.pallas_call(
         functools.partial(layer_kernel, seq_count, fsdp_count),
@@ -408,25 +519,25 @@
             held(*gate_weight.shape),
             held(*up_weight.shape),
             held(*down_weight.shape),
-            held(rows, kv_width),
             held(seq_count, rows, kv_width),
-            held(columns, w_rows),
             held(seq_count, columns, w_rows),
             held(KVH, HEADS // KVH * rows, HD),
             pltpu.VMEM((rows, seq_count * rows), jnp.float32),
             held(KVH, fsdp_count, rows, HEADS // KVH * HD),
             held(fsdp_count, rows, columns),
             held(fsdp_count, rows, columns),
-            held(EXPERTS, CAP, D),
-            held(seq_count, CAP, D),
+            held(EXPERTS, 2 * CAP, fold),
+            held(seq_count, 2 * CAP, fold),
             held(seq_count // 2 * CAP, D),
-            held(seq_count, CAP, D),
-            held(seq_count, CAP, D),
-            held(seq_count * CAP, D),
+            held(seq_count, 2 * CAP, fold),
+            held(seq_count, 2 * CAP, fold),
+            held(4 * rows, seq_count * 2 * CAP),
             dma((9,)),
         ]
-        + gather_sems
-        + gather_sems
+        + [dma((z_count,))] * 4
+        + [dma((2, z_count))] * 2
+        + [dma((2, z_count, 2)), dma((z_count, 2)), dma((z_count, 2)), dma((z_count, 2))]
+        + [dma((2, z_count, 2))] * 2
         + [dma((4,)), dma((KVH, fsdp_count)), dma((KVH, fsdp_count)), dma((fsdp_count,)), dma((fsdp_count,))]
         + [dma((seq_count,))] * 4,
         compiler_params=pltpu.CompilerParams(

time: 95.9 us -> 70.4 us (0.73)
  the two profiles are of different devices: /device:TPU:0 before, /device:TPU:11 now
where the time goes in v2:
time: 70.4 us; the launch traced here: 70.2 us
  Pallas kernels  67.8 us (96%)
  local copies, waits for them, and re-layouts  1.79 us (3%)
    pallas_call x1, Pallas kernels, on_device(): pl.pallas_call(functools.partial(layer_kernel, seq_count, fsdp_count), ou...  67.8 us
    slice x1, local copies, waits for them, and re-layouts, on_device(): return (both[0][None], both[1][None])  1.79 us

profile of v2, /device:TPU:11, one launch (start us, length us, event | category | flops | bytes accessed | tf_op | source)
XLA Modules:
  0.0 70.2 jit_solution(5593136216109756044)
XLA Ops:
  0.6 67.8 %shard_map.140 = bf16[2,64,1440]{2,1,0:T(8,128)(2,1)} custom-call(f32[1,32]{1,0:T(1,128)} %bitcast.18, s32[1,32]{1,0:T(1,128)} %bitcast.19, bf16[1440]{0:T(1024)(128)(2,1)} %gain_ref.1, s32[2,64]{1,0:T(2,128)} %bitcast.17, bf16[64,1440]{1,0:T(8,128)(2,1)} %bitcast.12, bf16[64,2048]{1,0:T(8,128)(2,1)} %bitcast.11, bf16[64,256]{1,0:T(8,128)(2,1)} %bitcast.15, ...), custom_call_target="tpu_custom_call" | custom-call | tf_op jit(solution)/shard_map/pallas_call | solution.py:508
  68.4 1.8 %fusion = (bf16[1,64,1440]{2,1,0:T(8,128)(2,1)}, bf16[1,64,1440]{2,1,0:T(8,128)(2,1)}) fusion(bf16[2,64,1440]{2,1,0:T(8,128)(2,1)} %shard_map.140), kind=kLoop, calls=%fused_computation | loop fusion | bytes 737280 | tf_op jit(solution)/shard_map/slice | solution.py:561

commit v3 on v2

--- a/solution.py
+++ b/solution.py
@@ -37,26 +37,28 @@
     )
 
 
-def greet(peers):
-    barrier = pltpu.get_barrier_semaphore()
-    for where in peers:
-        pl.semaphore_signal(barrier, inc=1, device_id=where, device_id_type=MESH)
-    pl.semaphore_wait(barrier, len(peers))
-
-
 def slot(z, y, c):
     return (z * 2 + y) * 2 + c
 
 
+def plane(far, j, z, z_count, sign=1):
+    reach = z_count // 2
+    base, inner = z // reach, lax.rem(z, reach)
+    step = lax.rem(inner + j, reach) if sign > 0 else lax.rem(inner + reach - j, reach)
+    return (1 - base if far else base) * reach + step
+
+
 def gather_plan(slots, sems, z_count, z, y, c):
     z_send, z_recv, y_send, y_recv, c_send, c_recv = sems
+    reach = z_count // 2
+    order = [(0, 0)] + [(1, j) for j in range(reach)] + [(0, j) for j in range(1, reach)]
 
     def z_of(d):
-        return lax.rem(z + z_count - d, z_count)
+        return plane(*order[d], z, z_count, sign=-1)
 
     own = slots.at[slot(z, y, c)]
     to_z = [
-        remote(own, own, z_send.at[d], z_recv.at[d], seq=slot(lax.rem(z + d, z_count), y, c))
+        remote(own, own, z_send.at[d], z_recv.at[d], seq=slot(plane(*order[d], z, z_count), y, c))
         for d in range(1, z_count)
     ]
 
@@ -101,31 +103,39 @@
     z_send, z_recv, y_send, y_recv, c_send, c_recv = sems
     last = z_count - 1
 
-    def block(zz, yy, p):
-        return slots.at[slot(zz, yy, c), pl.ds(*pieces[p])]
-
-    def along(way, zz, p):
-        part = block(zz, y, p)
-        return remote(part, part, z_send.at[way, zz, p], z_recv.at[zz, p], seq=slot(z + 1 - 2 * way, y, c))
+    def block(side, zz, p):
+        start, size, _ = pieces[p]
+        return slots.at[slot(zz, 1 - y if side else y, c), pl.ds(start, size)]
+
+    def along(way, side, zz, p):
+        part = block(side, zz, p)
+        return remote(
+            part, part, z_send.at[way, side, zz, p], z_recv.at[side, zz, p], seq=slot(z + 1 - 2 * way, y, c)
+        )
 
     def over(zz, p):
-        part = block(zz, y, p)
+        part = block(0, zz, p)
         return remote(part, part, y_send.at[zz, p], y_recv.at[zz, p], seq=slot(z, 1 - y, c))
 
     def beside(side, zz, p):
-        part = block(zz, 1 - y if side else y, p)
+        part = block(side, zz, p)
         return remote(part, part, c_send.at[side, zz, p], c_recv.at[side, zz, p], seq=slot(z, y, 1 - c))
 
-    def onward(way, zz, p):
+    def sides(p):
+        return range(2) if pieces[p][2] else range(1)
+
+    def onward(way, side, zz, p):
         @pl.when(z < last if way == 0 else z > 0)
         def _():
-            along(way, zz, p).start()
+            along(way, side, zz, p).start()
 
     def start(p):
-        onward(0, z, p)
-        onward(1, z, p)
+        onward(0, 0, z, p)
+        onward(1, 0, z, p)
+        beside(0, z, p).start()
+
+    def cross(p):
         over(z, p).start()
-        beside(0, z, p).start()
 
     def each(k, act):
         for way in range(2):
@@ -137,10 +147,12 @@
 
     def relay(k, p):
         def act(way, zz):
-            along(way, zz, p).wait_recv()
-            onward(way, zz, p)
-            over(zz, p).start()
-            beside(0, zz, p).start()
+            for side in sides(p):
+                along(way, side, zz, p).wait_recv()
+                onward(way, side, zz, p)
+                beside(side, zz, p).start()
+            if not pieces[p][2]:
+                over(zz, p).start()
 
         each(k, act)
 
@@ -148,63 +160,90 @@
         def act(way, zz):
             over(zz, p).wait_recv()
             beside(1, zz, p).start()
+            if pieces[p][2]:
+                onward(0, 1, zz, p)
+                onward(1, 1, zz, p)
 
         if k < 0:
             act(0, z)
         else:
             each(k, act)
 
-    every = [(zz, p) for zz in range(z_count) for p in range(len(pieces))]
-
-    def finish():
-        for zz, p in every:
+    def ready(zz):
+        for p in range(len(pieces)):
             for side in range(2):
                 beside(side, zz, p).wait_recv()
 
     def drain():
-        for zz, p in every:
-            @pl.when((z >= zz) & (z < last))
-            def _():
-                along(0, zz, p).wait_send()
-
-            @pl.when((z <= zz) & (z > 0))
-            def _():
-                along(1, zz, p).wait_send()
-
-            over(zz, p).wait_send()
-            for side in range(2):
-                beside(side, zz, p).wait_send()
-
-    return start, relay, across, finish, drain
+        for p in range(len(pieces)):
+            for zz in range(z_count):
+                for side in sides(p):
+                    @pl.when((z >= zz) & (z < last))
+                    def _():
+                        along(0, side, zz, p).wait_send()
+
+                    @pl.when((z <= zz) & (z > 0))
+                    def _():
+                        along(1, side, zz, p).wait_send()
+
+                if not pieces[p][2]:
+                    over(zz, p).wait_send()
+                for side in range(2):
+                    beside(side, zz, p).wait_send()
+            if pieces[p][2]:
+                over(z, p).wait_send()
+
+    return start, cross, relay, across, ready, drain
 
 
 def layer_kernel(
     seq_count, fsdp_count,
-    sink_ref, span_ref, gain_ref, routing_ref,
-    res_hbm, q_hbm, k_hbm, v_hbm, w_hbm, router_hbm, gate_hbm, up_hbm, down_hbm,
+    sink_hbm, span_hbm, gain_hbm, routing_hbm, res_hbm, q_hbm, k_hbm, v_hbm, w_hbm, router_hbm, gate_hbm, up_hbm, down_hbm,
     out_ref,
-    res, q_raw, k_raw, v_raw, router, gate, up, down,
+    sink_ref, span_ref, gain_ref, routing_ref, res, q_raw, k_raw, v_raw, router, gate, up, down,
     kv_all, w_all, q_rot, bias, rows_all, proj, got,
-    x_out, arrived, stacked, back, returned, mix,
+    x_out, arrived, stacked, back, returned, mix, dispatch,
     load_sems,
-    kzs, kzr, kys, kyr, kcs, kcr, wzs, wzr, wys, wyr, wcs, wcr, own_sems, as_, ar, ps, pr,
+    kzs, kzr, kys, kyr, kcs, kcr, wzs, wzr, wys, wyr, wcs, wcr, as_, ar, ps, pr,
     xs, xr, bs, br,
 ):
     me = lax.axis_index("seq")
     f_me = lax.axis_index("fsdp")
-    sources = (k_hbm, v_hbm, w_hbm, q_hbm, res_hbm, router_hbm, gate_hbm, up_hbm, down_hbm)
-    targets = (k_raw, v_raw, w_all.at[me], q_raw, res, router, gate, up, down)
+    sources = (
+        k_hbm, v_hbm, w_hbm, q_hbm, res_hbm, router_hbm, gate_hbm, up_hbm, down_hbm,
+        span_hbm, sink_hbm, routing_hbm, gain_hbm,
+    )
+    targets = (
+        k_raw, v_raw, w_all.at[me], q_raw, res, router, gate, up, down, span_ref, sink_ref, routing_ref, gain_ref,
+    )
     loads = [
         pltpu.make_async_copy(a, b, load_sems.at[i]) for i, (a, b) in enumerate(zip(sources, targets))
     ]
-    for load in loads[:6]:
+    for load in loads[9:] + loads[:6]:
         load.start()
 
     z_count = seq_count // 4
     z, y, c = me // 4, lax.rem(me // 2, 2), lax.rem(me, 2)
+    reach = z_count // 2
+
+    def peer_of(far, j, side, cc, sign=1):
+        zz = plane(far, j, z, z_count, sign)
+        return (zz * 2 + (1 - y if side else y)) * 2 + (1 - c if cc else c)
+
+    relative = [
+        (far, j, side, cc) for far in range(2) for j in range(reach) for side in range(2) for cc in range(2)
+    ]
+    peers = [{"seq": peer_of(*r)} for r in relative[1:]]
+    peers += [{"fsdp": lax.rem(f_me + d, fsdp_count)} for d in range(1, fsdp_count)]
+    barrier = pltpu.get_barrier_semaphore()
+    for where in peers:
+        pl.semaphore_signal(barrier, inc=1, device_id=where, device_id_type=MESH)
+
     rows, key_count = bias.shape
     group_size = HEADS // KVH
     copies = seq_count // EXPERTS
+
+    loads[9].wait()
 
     def spot(row):
         return jnp.where(row < HALF, span_ref[0, 2 * me], span_ref[0, 2 * me + 1]) * HALF + row % HALF
@@ -228,30 +267,23 @@
     keys = [rotated(k_raw[:, i * 2 * HD:(i + 1) * 2 * HD]) for i in range(KVH // 2)]
     kv_all[pl.ds(me, 1)] = jnp.concatenate(keys + [v_raw[...]], axis=1)[None]
 
-    reach = z_count // 2
-    base, inner = z // reach, lax.rem(z, reach)
-
-    def peer_of(far, j, side, cc, sign=1):
-        step = lax.rem(inner + j, reach) if sign > 0 else lax.rem(inner + reach - j, reach)
-        zz = (1 - base if far else base) * reach + step
-        return (zz * 2 + (1 - y if side else y)) * 2 + (1 - c if cc else c)
-
-    relative = [
-        (far, j, side, cc) for far in range(2) for j in range(reach) for side in range(2) for cc in range(2)
-    ]
-    peers = [{"seq": peer_of(*r)} for r in relative[1:]]
-    peers += [{"fsdp": lax.rem(f_me + d, fsdp_count)} for d in range(1, fsdp_count)]
-    greet(peers)
+    pl.semaphore_wait(barrier, len(peers))
 
     w_columns, w_rows = w_all.shape[1:]
-    cut = w_columns // 32 * 16
-    pieces = [(0, cut), (cut, w_columns - cut)] if w_columns % 16 == 0 else [(0, w_columns)]
+    pieces = [(0, w_columns, False)]
+    if w_columns % 16 == 0:
+        cut = w_columns // 40 * 16
+        pieces = [(0, cut, False), (cut, cut, False), (2 * cut, w_columns - 2 * cut, True)]
+    plain = [p for p in range(len(pieces)) if not pieces[p][2]]
+    turned = [p for p in range(len(pieces)) if pieces[p][2]]
     kv = gather_plan(kv_all, (kzs, kzr, kys, kyr, kcs, kcr), z_count, z, y, c)
     w = line_plan(w_all, pieces, (wzs, wzr, wys, wyr, wcs, wcr), z_count, z, y, c)
     kv[0]()
     kv[1](0)
     loads[2].wait()
-    for p in range(len(pieces)):
+    for p in turned + plain[:1]:
+        w[1](p)
+    for p in plain + turned:
         w[0](p)
     loads[3].wait()
     for i in range(HEADS // 2):
@@ -267,6 +299,8 @@
     query_at = spot(lax.broadcasted_iota(jnp.int32, (rows, 1), 0))
     bias[...] = jnp.where(key_at <= query_at, 0.0, masked_score)
 
+    for load in loads[10:]:
+        load.wait()
     chosen = routing_ref[...]
     expert_row = lax.broadcasted_iota(jnp.int32, (EXPERTS, rows), 0)
     picks = [chosen[j:j + 1, :] == expert_row for j in range(TOPK)]
@@ -279,23 +313,38 @@
         jnp.sum(jnp.where(p, before, 0.0), axis=0, keepdims=True).astype(jnp.int32) for p in picks
     ]
 
+    column = lax.broadcasted_iota(jnp.int32, (1, 2 * rows), 1)
+    wrap = column // rows
+    chosen_twice = jnp.concatenate([chosen, chosen], axis=1)
+    slot_twice = [jnp.concatenate([slots[j], slots[j]], axis=1) for j in range(TOPK)]
+    place = lax.broadcasted_iota(jnp.int32, (EXPERTS * 2 * CAP, 2 * rows), 0)
+    dispatch[...] = sum(
+        (place == chosen_twice[j:j + 1, :] * (2 * CAP) + wrap * CAP + slot_twice[j]).astype(jnp.float32)
+        for j in range(TOPK)
+    ).astype(jnp.bfloat16)
+
     for d in range(1, z_count):
         kv[1](d)
-    for load in loads[6:]:
+        if d == 1:
+            for p in turned:
+                w[3](-1, p)
+    for load in loads[6:9]:
         load.start()
-    steps = [functools.partial(w[1], 0, p) for p in range(len(pieces))]
-    steps += [functools.partial(w[2], -1, p) for p in range(len(pieces))]
-    for k in range(1, z_count - 1):
-        for p in range(len(pieces)):
-            steps += [functools.partial(w[1], k, p), functools.partial(w[2], k - 1, p)]
-    closing = [functools.partial(w[2], z_count - 2, p) for p in range(len(pieces))]
-    early = len(pieces)
-    steps.pop(0)()
+    for p in plain[1:]:
+        w[1](p)
+    for p in plain:
+        w[2](0, p)
     for d in range(z_count):
         kv[2](d)
-    for _ in range(early - 1):
-        steps.pop(0)()
+    w[3](-1, plain[0])
     kv[3]()
+    steps = [functools.partial(w[3], -1, p) for p in plain[1:]]
+    steps += [functools.partial(w[2], 0, p) for p in turned]
+    for k in range(1, z_count - 1):
+        for p in plain:
+            steps += [functools.partial(w[2], k, p), functools.partial(w[3], k - 1, p)]
+        steps += [functools.partial(w[2], k, p) for p in turned]
+    closing = [functools.partial(w[3], z_count - 2, p) for p in plain]
 
     chunk = 4
 
@@ -310,7 +359,7 @@
 
     row_copies = [send_rows(g) for g in range(KVH)]
     turns = KVH * group_size // chunk
-    share = -(-len(steps) // turns)
+    share = max(1, len(steps) // turns)
     for g in range(KVH):
         keys = kv_all[:, :, g * HD:(g + 1) * HD].reshape(key_count, HD)
         vals = kv_all[:, :, (KVH + g) * HD:(KVH + g + 1) * HD].reshape(key_count, HD)
@@ -329,27 +378,32 @@
             o = jnp.dot(jnp.concatenate(weights, axis=0), vals, preferred_element_type=jnp.float32)
             for i in range(chunk):
                 parts.append((o[i * rows:(i + 1) * rows, :] / totals[i]).astype(jnp.bfloat16))
-            if part == 0 and g > 0:
-                for copy in row_copies[g - 1]:
+            if part == group_size // chunk - 1:
+                rows_all[g, pl.ds(f_me, 1)] = jnp.concatenate(parts, axis=1)[None]
+                for copy in row_copies[g]:
                     copy.start()
             for step in steps[:share]:
                 step()
             steps = steps[share:]
-        rows_all[g, pl.ds(f_me, 1)] = jnp.concatenate(parts, axis=1)[None]
-    for copy in row_copies[KVH - 1]:
-        copy.start()
-    for step in steps + closing:
+    for step in steps:
         step()
     loads[4].wait()
     loads[5].wait()
-    w[3]()
 
     width = group_size * HD
     count = width // w_rows
     pair = max(1, 256 // w_rows)
+    upward = list(range(KVH))
+    downward = [*range(KVH - 2, 0, -1), KVH - 1, 0]
     total = None
-    for g in range(KVH):
-        for copy in row_copies[g]:
+    for i in range(KVH):
+        g = jnp.where(z < z_count // 2, upward[i], downward[i])
+        if i == KVH - 1:
+            for step in closing:
+                step()
+        for zz in range(z_count // KVH):
+            w[4](g * (z_count // KVH) + zz)
+        for copy in send_rows(g):
             copy.wait_recv()
         for first in range(0, count, pair):
             block = jnp.concatenate([w_all[g * count + first + i] for i in range(pair)], axis=1)
@@ -367,9 +421,45 @@
         backs.append(remote(proj.at[peer], got.at[f_me], ps.at[d], pr.at[d], fsdp=peer))
     for copy in backs:
         copy.start()
+
+    shares, thin = x_out.shape[0], x_out.shape[3]
+    widths = [w_columns, D - w_columns] if shares == 2 else [D]
+
+    def share_of(t, wide):
+        if shares == 1:
+            return wide
+        return jnp.where(f_me == t, wide[:, :w_columns], wide[:, w_columns:])
+
+    def rows_of(t, weight):
+        if shares == 1:
+            return weight[...]
+        return weight[pl.ds((f_me if t == 0 else 1 - f_me) * w_columns, w_columns), :]
+
+    sends, returns = [{} for _ in range(shares)], {}
+    for r, rel in enumerate(relative[1:], 1):
+        to, source = peer_of(*rel), peer_of(*rel, sign=-1)
+        for t in range(shares):
+            sends[t][r] = remote(
+                x_out.at[t, to // copies], arrived.at[t, r], xs.at[t, r], xr.at[t, r], seq=to
+            )
+        returns[r] = remote(back.at[r], returned.at[me], bs.at[r], br.at[r], seq=source)
+
+    def send_share(t, scaled, tail):
+        full = jnp.concatenate([scaled, tail], axis=1).astype(jnp.bfloat16)
+        both = jnp.concatenate([full[:, :thin], full[:, thin:]], axis=0)
+        buffer = jnp.dot(dispatch[...], both, preferred_element_type=jnp.float32).astype(jnp.bfloat16)
+        for e in range(EXPERTS):
+            x_out[t, e] = buffer[e * 2 * CAP:(e + 1) * 2 * CAP, :]
+        for copy in sends[t].values():
+            copy.start()
+
+    gain = gain_ref[...][None, :].astype(jnp.float32)
+    if shares == 2:
+        local = share_of(0, res[...].astype(jnp.float32)) + proj[f_me].astype(jnp.float32)
+        send_share(0, local * share_of(0, gain), jnp.zeros((rows, 2 * thin - w_columns), jnp.float32))
     got[pl.ds(f_me, 1)] = proj[pl.ds(f_me, 1)]
     kv[4]()
-    w[4]()
+    w[5]()
     for g in range(KVH):
         for copy in row_copies[g]:
             copy.wait_send()
@@ -381,43 +471,19 @@
         copy.wait_send()
 
     stream = res[...].astype(jnp.float32) + out_ref[0].astype(jnp.float32)
-    normed = (
-        stream
-        * lax.rsqrt(jnp.mean(stream * stream, axis=-1, keepdims=True) + norm_eps)
-        * gain_ref[...][None, :].astype(jnp.float32)
-    ).astype(jnp.bfloat16)
-    fold = x_out.shape[2]
+    scale = lax.rsqrt(jnp.mean(stream * stream, axis=-1, keepdims=True) + norm_eps)
+    scale_high = scale.astype(jnp.bfloat16).astype(jnp.float32)
+    tail_lane = lax.broadcasted_iota(jnp.int32, (rows, 2 * thin - widths[-1]), 1)
+    tail = jnp.where(tail_lane == 0, scale_high, jnp.where(tail_lane == 1, scale - scale_high, 0.0))
+    send_share(shares - 1, share_of(1, stream * gain), tail)
+    normed = (stream * scale * gain).astype(jnp.bfloat16)
+
+    fold = back.shape[2]
     spare = 2 * fold - D
-    column = lax.broadcasted_iota(jnp.int32, (1, 2 * rows), 1)
-    wrap = column // rows
-    chosen_twice = jnp.concatenate([chosen, chosen], axis=1)
-    slot_twice = [jnp.concatenate([slots[j], slots[j]], axis=1) for j in range(TOPK)]
-    place = lax.broadcasted_iota(jnp.int32, (EXPERTS * 2 * CAP, 2 * rows), 0)
-    dispatch = sum(
-        (place == chosen_twice[j:j + 1, :] * (2 * CAP) + wrap * CAP + slot_twice[j]).astype(jnp.float32)
-        for j in range(TOPK)
-    ).astype(jnp.bfloat16)
 
     def folded(wide):
         right = jnp.concatenate([wide[:, fold:], jnp.zeros((wide.shape[0], spare), wide.dtype)], axis=1)
         return wide[:, :fold], right
-
-    buffer = jnp.dot(
-        dispatch, jnp.concatenate(folded(normed), axis=0), preferred_element_type=jnp.float32
-    ).astype(jnp.bfloat16)
-    for e in range(EXPERTS):
-        x_out[e] = buffer[e * 2 * CAP:(e + 1) * 2 * CAP, :]
-
-    sends, returns = {}, {}
-    for r, rel in enumerate(relative[1:], 1):
-        to, source = peer_of(*rel), peer_of(*rel, sign=-1)
-        sends[r] = remote(x_out.at[to // copies], arrived.at[r], xs.at[r], xr.at[r], seq=to)
-        returns[r] = remote(back.at[r], returned.at[me], bs.at[r], br.at[r], seq=source)
-    own = pltpu.make_async_copy(x_out.at[me // copies], arrived.at[0], own_sems.at[2])
-    keep = pltpu.make_async_copy(back.at[0], returned.at[me], own_sems.at[3])
-    for copy in sends.values():
-        copy.start()
-    own.start()
 
     logits = lax.dot_general(
         router[...], normed, (((1,), (1,)), ((), ())), preferred_element_type=jnp.float32
@@ -438,32 +504,42 @@
     coarse = mixing.astype(jnp.bfloat16).astype(jnp.float32)
     mix[...] = jnp.concatenate([coarse, mixing - coarse], axis=1).T.astype(jnp.bfloat16)
 
-    for load in loads[6:]:
+    for load in loads[6:9]:
         load.wait()
     near = len(relative) // 2
     chunks = [range(near), range(near, near + near // 2), range(near + near // 2, 2 * near)]
     for chunk in chunks:
-        for i, r in enumerate(chunk):
-            sends[r].wait_recv() if r > 0 else own.wait()
-            block = arrived[r]
-            stacked[i * CAP:(i + 1) * CAP, :fold] = block[:CAP, :]
-            stacked[i * CAP:(i + 1) * CAP, fold:] = block[CAP:, :D - fold]
-        x = stacked[:len(chunk) * CAP, :]
-        g = jnp.dot(x, gate[...], preferred_element_type=jnp.float32)
-        u = jnp.dot(x, up[...], preferred_element_type=jnp.float32)
+        g = u = 0.0
+        count = len(chunk) * CAP
+        for t in range(shares):
+            for i, r in enumerate(chunk):
+                if r > 0:
+                    sends[t][r].wait_recv()
+                    block = arrived[t, r]
+                else:
+                    block = x_out[t, me // copies]
+                stacked[t, i * CAP:(i + 1) * CAP, :thin] = block[:CAP, :]
+                stacked[t, i * CAP:(i + 1) * CAP, thin:] = block[CAP:, :]
+            x = stacked[t, :count, :widths[t]]
+            g = g + jnp.dot(x, rows_of(t, gate), preferred_element_type=jnp.float32)
+            u = u + jnp.dot(x, rows_of(t, up), preferred_element_type=jnp.float32)
+        scales = stacked[shares - 1, :count, widths[-1]:widths[-1] + 2].astype(jnp.float32)
+        scales = scales[:, :1] + scales[:, 1:]
+        g, u = g * scales, u * scales
         hidden = (g * jax.nn.sigmoid(1.702 * g) * (u + 1.0)).astype(jnp.bfloat16)
         part = jnp.dot(hidden, down[...], preferred_element_type=jnp.float32).astype(jnp.bfloat16)
         left, right = folded(part)
         for i, r in enumerate(chunk):
-            back[r, :CAP] = left[i * CAP:(i + 1) * CAP, :]
-            back[r, CAP:] = right[i * CAP:(i + 1) * CAP, :]
-        for r in chunk:
-            returns[r].start() if r > 0 else keep.start()
-    for copy in sends.values():
-        copy.wait_send()
+            target = back.at[r] if r > 0 else returned.at[me]
+            target[:CAP] = left[i * CAP:(i + 1) * CAP, :]
+            target[CAP:] = right[i * CAP:(i + 1) * CAP, :]
+            if r > 0:
+                returns[r].start()
+    for share in sends:
+        for copy in share.values():
+            copy.wait_send()
     for copy in returns.values():
         copy.wait_recv()
-    keep.wait()
     parts = jnp.dot(
         mix[...], returned[...].reshape(seq_count * 2 * CAP, fold), preferred_element_type=jnp.float32
     )
@@ -496,8 +572,7 @@
     rows = residual.shape[1]
     dma = pltpu.SemaphoreType.DMA
     vmem = pl.BlockSpec(memory_space=pltpu.VMEM)
-    smem = pl.BlockSpec(memory_space=pltpu.SMEM)
-    hbm = pl.BlockSpec(memory_space=pl.ANY)
+    hbm = pl.BlockSpec(memory_space=pltpu.HBM)
 
     def held(*shape):
         return pltpu.VMEM(shape, jnp.bfloat16)
@@ -505,12 +580,18 @@
     kv_width = 2 * KVH * HD
     fold = -(-D // 256) * 128
     w_rows, columns = out_weight.shape
+    shares = 2 if fsdp_count == 2 and columns % 16 == 0 else 1
+    thin = -(-((columns if shares == 2 else D) + 2) // 256) * 128
     both = pl.pallas_call(
         functools.partial(layer_kernel, seq_count, fsdp_count),
         out_shape=jax.ShapeDtypeStruct((2, rows, D), jnp.bfloat16),
-        in_specs=[smem, smem, vmem, vmem] + [hbm] * 9,
+        in_specs=[hbm] * 13,
         out_specs=vmem,
         scratch_shapes=[
+            pltpu.SMEM((1, HEADS), jnp.float32),
+            pltpu.SMEM((1, span_order.shape[0]), jnp.int32),
+            held(D),
+            pltpu.VMEM((TOPK, rows), jnp.int32),
             held(rows, D),
             held(rows, HEADS * HD),
             held(rows, KVH * HD),
@@ -526,20 +607,22 @@
             held(KVH, fsdp_count, rows, HEADS // KVH * HD),
             held(fsdp_count, rows, columns),
             held(fsdp_count, rows, columns),
-            held(EXPERTS, 2 * CAP, fold),
-            held(seq_count, 2 * CAP, fold),
-            held(seq_count // 2 * CAP, D),
+            held(shares, EXPERTS, 2 * CAP, thin),
+            held(shares, seq_count, 2 * CAP, thin),
+            held(shares, seq_count // 2 * CAP, 2 * thin),
             held(seq_count, 2 * CAP, fold),
             held(seq_count, 2 * CAP, fold),
             held(4 * rows, seq_count * 2 * CAP),
-            dma((9,)),
+            held(EXPERTS * 2 * CAP, 2 * rows),
+            dma((13,)),
         ]
         + [dma((z_count,))] * 4
         + [dma((2, z_count))] * 2
-        + [dma((2, z_count, 2)), dma((z_count, 2)), dma((z_count, 2)), dma((z_count, 2))]
-        + [dma((2, z_count, 2))] * 2
-        + [dma((4,)), dma((KVH, fsdp_count)), dma((KVH, fsdp_count)), dma((fsdp_count,)), dma((fsdp_count,))]
-        + [dma((seq_count,))] * 4,
+        + [dma((2, 2, z_count, 3)), dma((2, z_count, 3)), dma((z_count, 3)), dma((z_count, 3))]
+        + [dma((2, z_count, 3))] * 2
+        + [dma((KVH, fsdp_count)), dma((KVH, fsdp_count)), dma((fsdp_count,)), dma((fsdp_count,))]
+        + [dma((shares, seq_count))] * 2
+        + [dma((seq_count,))] * 2,
         compiler_params=pltpu.CompilerParams(
             collective_id=0, has_side_effects=True, vmem_limit_bytes=60 * 1024 * 1024
         ),

time: 70.4 us -> 66.8 us (0.949)
  the two profiles are of different devices: /device:TPU:11 before, /device:TPU:0 now
where the time goes in v3:
time: 66.8 us; the launch traced here: 65.6 us
  Pallas kernels  63.2 us (95%)
  local copies, waits for them, and re-layouts  1.79 us (3%)
    pallas_call x1, Pallas kernels, on_device(): pl.pallas_call(functools.partial(layer_kernel, seq_count, fsdp_count), ou...  63.2 us
    slice x1, local copies, waits for them, and re-layouts, on_device(): return (both[0][None], both[1][None])  1.79 us

profile of v3, /device:TPU:0, one launch (start us, length us, event | category | flops | bytes accessed | tf_op | source)
XLA Modules:
  0.0 65.6 jit_solution(8412775248116977289)
XLA Ops:
  0.6 63.2 %shard_map.140 = bf16[2,64,1440]{2,1,0:T(8,128)(2,1)} custom-call(f32[1,32]{1,0:T(1,128)} %bitcast.18, s32[1,32]{1,0:T(1,128)} %bitcast.19, bf16[1440]{0:T(1024)(128)(2,1)} %gain_hbm.1, s32[2,64]{1,0:T(2,128)} %bitcast.17, bf16[64,1440]{1,0:T(8,128)(2,1)} %bitcast.12, bf16[64,2048]{1,0:T(8,128)(2,1)} %bitcast.11, bf16[64,256]{1,0:T(8,128)(2,1)} %bitcast.15, ...), custom_call_target="tpu_custom_call" | custom-call | tf_op jit(solution)/shard_map/pallas_call | solution.py:585
  63.8 1.8 %fusion = (bf16[1,64,1440]{2,1,0:T(8,128)(2,1)}, bf16[1,64,1440]{2,1,0:T(8,128)(2,1)}) fusion(bf16[2,64,1440]{2,1,0:T(8,128)(2,1)} %shard_map.140), kind=kLoop, calls=%fused_computation | loop fusion | bytes 737280 | tf_op jit(solution)/shard_map/slice | solution.py:644

commit v4 on v3

--- a/solution.py
+++ b/solution.py
@@ -37,6 +37,13 @@
     )
 
 
+KV_SENT, KV_BESIDE, W_OVER, W_TURNED, W_BESIDE, ROWS_SENT, X_SENT, BACK_SENT, BACK_HERE = range(9)
+
+
+def settle(as_large, sem):
+    pltpu.make_async_copy(as_large, as_large, sem).wait()
+
+
 def slot(z, y, c):
     return (z * 2 + y) * 2 + c
 
@@ -49,7 +56,7 @@
 
 
 def gather_plan(slots, sems, z_count, z, y, c):
-    z_send, z_recv, y_send, y_recv, c_send, c_recv = sems
+    z_recv, y_recv, once = sems
     reach = z_count // 2
     order = [(0, 0)] + [(1, j) for j in range(reach)] + [(0, j) for j in range(1, reach)]
 
@@ -58,17 +65,17 @@
 
     own = slots.at[slot(z, y, c)]
     to_z = [
-        remote(own, own, z_send.at[d], z_recv.at[d], seq=slot(plane(*order[d], z, z_count), y, c))
+        remote(own, own, once.at[KV_SENT], z_recv.at[d], seq=slot(plane(*order[d], z, z_count), y, c))
         for d in range(1, z_count)
     ]
 
     def to_y(d):
         block = slots.at[slot(z_of(d), y, c)]
-        return remote(block, block, y_send.at[d], y_recv.at[d], seq=slot(z, 1 - y, c))
+        return remote(block, block, once.at[KV_SENT], y_recv.at[d], seq=slot(z, 1 - y, c))
 
     def to_c(side, d):
         block = slots.at[slot(z_of(d), y if side == 0 else 1 - y, c)]
-        return remote(block, block, c_send.at[side, d], c_recv.at[side, d], seq=slot(z, y, 1 - c))
+        return remote(block, block, once.at[KV_SENT], once.at[KV_BESIDE], seq=slot(z, y, 1 - c))
 
     ys = [to_y(d) for d in range(z_count)]
     cs = [[to_c(side, d) for d in range(z_count)] for side in range(2)]
@@ -88,19 +95,16 @@
         cs[1][d].start()
 
     def finish():
-        for side in range(2):
-            for d in range(z_count):
-                cs[side][d].wait_recv()
+        settle(slots.at[pl.ds(0, 2 * z_count)], once.at[KV_BESIDE])
 
     def drain():
-        for copy in to_z + ys + cs[0] + cs[1]:
-            copy.wait_send()
+        settle(slots.at[pl.ds(0, 4 * z_count - 1)], once.at[KV_SENT])
 
     return start_z, relay, relay_across, finish, drain
 
 
 def line_plan(slots, pieces, sems, z_count, z, y, c):
-    z_send, z_recv, y_send, y_recv, c_send, c_recv = sems
+    z_send, z_recv, y_recv, c_recv, once = sems
     last = z_count - 1
 
     def block(side, zz, p):
@@ -109,17 +113,18 @@
 
     def along(way, side, zz, p):
         part = block(side, zz, p)
-        return remote(
-            part, part, z_send.at[way, side, zz, p], z_recv.at[side, zz, p], seq=slot(z + 1 - 2 * way, y, c)
-        )
+        lane = len(pieces) if side else p
+        sent = jnp.where((zz == z) & (way == 1), z_count, zz)
+        return remote(part, part, z_send.at[sent, lane], z_recv.at[zz, lane], seq=slot(z + 1 - 2 * way, y, c))
 
     def over(zz, p):
         part = block(0, zz, p)
-        return remote(part, part, y_send.at[zz, p], y_recv.at[zz, p], seq=slot(z, 1 - y, c))
+        sent = once.at[W_TURNED if pieces[p][2] else W_OVER]
+        return remote(part, part, sent, y_recv.at[zz, p], seq=slot(z, 1 - y, c))
 
     def beside(side, zz, p):
         part = block(side, zz, p)
-        return remote(part, part, c_send.at[side, zz, p], c_recv.at[side, zz, p], seq=slot(z, y, 1 - c))
+        return remote(part, part, once.at[W_BESIDE], c_recv.at[zz], seq=slot(z, y, 1 - c))
 
     def sides(p):
         return range(2) if pieces[p][2] else range(1)
@@ -170,9 +175,7 @@
             each(k, act)
 
     def ready(zz):
-        for p in range(len(pieces)):
-            for side in range(2):
-                beside(side, zz, p).wait_recv()
+        settle(slots.at[pl.ds(0, 2)], c_recv.at[zz])
 
     def drain():
         for p in range(len(pieces)):
@@ -186,12 +189,11 @@
                     def _():
                         along(1, side, zz, p).wait_send()
 
-                if not pieces[p][2]:
-                    over(zz, p).wait_send()
-                for side in range(2):
-                    beside(side, zz, p).wait_send()
             if pieces[p][2]:
                 over(z, p).wait_send()
+        straight = sum(size for _, size, turned in pieces if not turned)
+        settle(slots.at[pl.ds(0, z_count), pl.ds(0, straight)], once.at[W_OVER])
+        settle(slots.at[pl.ds(0, 2 * z_count)], once.at[W_BESIDE])
 
     return start, cross, relay, across, ready, drain
 
@@ -202,10 +204,9 @@
     out_ref,
     sink_ref, span_ref, gain_ref, routing_ref, res, q_raw, k_raw, v_raw, router, gate, up, down,
     kv_all, w_all, q_rot, bias, rows_all, proj, got,
-    x_out, arrived, stacked, back, returned, mix, dispatch,
+    x_out, arrived, stacked, begun, back, returned, mix, dispatch,
     load_sems,
-    kzs, kzr, kys, kyr, kcs, kcr, wzs, wzr, wys, wyr, wcs, wcr, as_, ar, ps, pr,
-    xs, xr, bs, br,
+    kzr, kyr, wzs, wzr, wyr, wcr, ar, ps, pr, xr, once,
 ):
     me = lax.axis_index("seq")
     f_me = lax.axis_index("fsdp")
@@ -276,8 +277,8 @@
         pieces = [(0, cut, False), (cut, cut, False), (2 * cut, w_columns - 2 * cut, True)]
     plain = [p for p in range(len(pieces)) if not pieces[p][2]]
     turned = [p for p in range(len(pieces)) if pieces[p][2]]
-    kv = gather_plan(kv_all, (kzs, kzr, kys, kyr, kcs, kcr), z_count, z, y, c)
-    w = line_plan(w_all, pieces, (wzs, wzr, wys, wyr, wcs, wcr), z_count, z, y, c)
+    kv = gather_plan(kv_all, (kzr, kyr, once), z_count, z, y, c)
+    w = line_plan(w_all, pieces, (wzs, wzr, wyr, wcr, once), z_count, z, y, c)
     kv[0]()
     kv[1](0)
     loads[2].wait()
@@ -337,34 +338,47 @@
     for d in range(z_count):
         kv[2](d)
     w[3](-1, plain[0])
+    for p in turned:
+        w[2](0, p)
     kv[3]()
-    steps = [functools.partial(w[3], -1, p) for p in plain[1:]]
-    steps += [functools.partial(w[2], 0, p) for p in turned]
-    for k in range(1, z_count - 1):
-        for p in plain:
-            steps += [functools.partial(w[2], k, p), functools.partial(w[3], k - 1, p)]
-        steps += [functools.partial(w[2], k, p) for p in turned]
-    closing = [functools.partial(w[3], z_count - 2, p) for p in plain]
 
     chunk = 4
 
-    def send_rows(g):
+    halves = group_size // chunk
+
+    def send_rows(g, part):
+        columns = rows_all.at[g, f_me, :, pl.ds(part * chunk * HD, chunk * HD)]
         return [
             remote(
-                rows_all.at[g, f_me], rows_all.at[g, f_me], as_.at[g, d], ar.at[g, d],
-                fsdp=lax.rem(f_me + d, fsdp_count),
+                columns, columns, once.at[ROWS_SENT], ar.at[g, part, d - 1], fsdp=lax.rem(f_me + d, fsdp_count)
             )
             for d in range(1, fsdp_count)
         ]
 
-    row_copies = [send_rows(g) for g in range(KVH)]
     turns = KVH * group_size // chunk
-    share = max(1, len(steps) // turns)
+    agenda = [[] for _ in range(turns)]
+
+    def plan(turn, act, k, p):
+        agenda[min(turn, turns - 1)].append(functools.partial(act, k, p))
+
+    for p in plain[1:]:
+        plan(0, w[3], -1, p)
+    for k in range(1, z_count - 1):
+        for i, p in enumerate(plain):
+            if k == 1 and i == 0:
+                w[2](k, p)
+            else:
+                plan(3 * (k - 1) + max(i - (k == 1), 0), w[2], k, p)
+        for p in turned:
+            plan(3 * k - 1, w[2], k, p)
+        for i, p in enumerate(plain):
+            plan(3 * k + 1 + i, w[3], k - 1, p)
+    closing = [functools.partial(w[3], z_count - 2, p) for p in plain]
     for g in range(KVH):
         keys = kv_all[:, :, g * HD:(g + 1) * HD].reshape(key_count, HD)
         vals = kv_all[:, :, (KVH + g) * HD:(KVH + g + 1) * HD].reshape(key_count, HD)
-        parts = []
-        for part in range(group_size // chunk):
+        for part in range(halves):
+            parts = []
             q = q_rot[g, part * chunk * rows:(part + 1) * chunk * rows, :]
             s = lax.dot_general(q, keys, (((1,), (1,)), ((), ())), preferred_element_type=jnp.float32)
             weights, totals = [], []
@@ -378,15 +392,11 @@
             o = jnp.dot(jnp.concatenate(weights, axis=0), vals, preferred_element_type=jnp.float32)
             for i in range(chunk):
                 parts.append((o[i * rows:(i + 1) * rows, :] / totals[i]).astype(jnp.bfloat16))
-            if part == group_size // chunk - 1:
-                rows_all[g, pl.ds(f_me, 1)] = jnp.concatenate(parts, axis=1)[None]
-                for copy in row_copies[g]:
-                    copy.start()
-            for step in steps[:share]:
+            rows_all[g, f_me, :, part * chunk * HD:(part + 1) * chunk * HD] = jnp.concatenate(parts, axis=1)
+            for copy in send_rows(g, part):
+                copy.start()
+            for step in agenda.pop(0):
                 step()
-            steps = steps[share:]
-    for step in steps:
-        step()
     loads[4].wait()
     loads[5].wait()
 
@@ -398,13 +408,14 @@
     total = None
     for i in range(KVH):
         g = jnp.where(z < z_count // 2, upward[i], downward[i])
-        if i == KVH - 1:
+        if i == 2 or (i == KVH - 1 and i < 2):
             for step in closing:
                 step()
         for zz in range(z_count // KVH):
             w[4](g * (z_count // KVH) + zz)
-        for copy in send_rows(g):
-            copy.wait_recv()
+        for part in range(halves):
+            for copy in send_rows(g, part):
+                copy.wait_recv()
         for first in range(0, count, pair):
             block = jnp.concatenate([w_all[g * count + first + i] for i in range(pair)], axis=1)
             term = lax.dot_general(
@@ -435,14 +446,21 @@
             return weight[...]
         return weight[pl.ds((f_me if t == 0 else 1 - f_me) * w_columns, w_columns), :]
 
+    near = len(relative) // 2
+    chunks = [range(near, near + near // 2), range(near + near // 2, 2 * near), range(near)]
+    far_first = [r for chunk in chunks for r in chunk]
+    chunk_of = {r: i for i, chunk in enumerate(chunks) for r in chunk}
     sends, returns = [{} for _ in range(shares)], {}
     for r, rel in enumerate(relative[1:], 1):
         to, source = peer_of(*rel), peer_of(*rel, sign=-1)
         for t in range(shares):
             sends[t][r] = remote(
-                x_out.at[t, to // copies], arrived.at[t, r], xs.at[t, r], xr.at[t, r], seq=to
+                x_out.at[t, to // copies], arrived.at[t, r], once.at[X_SENT], xr.at[t, chunk_of[r]], seq=to
             )
-        returns[r] = remote(back.at[r], returned.at[me], bs.at[r], br.at[r], seq=source)
+        returns[r] = remote(back.at[r], returned.at[me], once.at[BACK_SENT], once.at[BACK_HERE], seq=source)
+
+    late = [r for chunk in chunks for r in chunk if r > 0]
+    early = late[:near // 2 + near // 4] if shares == 2 else []
 
     def send_share(t, scaled, tail):
         full = jnp.concatenate([scaled, tail], axis=1).astype(jnp.bfloat16)
@@ -450,8 +468,15 @@
         buffer = jnp.dot(dispatch[...], both, preferred_element_type=jnp.float32).astype(jnp.bfloat16)
         for e in range(EXPERTS):
             x_out[t, e] = buffer[e * 2 * CAP:(e + 1) * 2 * CAP, :]
-        for copy in sends[t].values():
-            copy.start()
+        if t < shares - 1:
+            for r in early:
+                sends[t][r].start()
+            return
+        for r in late:
+            for other in range(shares - 1):
+                if r not in early:
+                    sends[other][r].start()
+            sends[t][r].start()
 
     gain = gain_ref[...][None, :].astype(jnp.float32)
     if shares == 2:
@@ -460,9 +485,8 @@
     got[pl.ds(f_me, 1)] = proj[pl.ds(f_me, 1)]
     kv[4]()
     w[5]()
-    for g in range(KVH):
-        for copy in row_copies[g]:
-            copy.wait_send()
+    if fsdp_count > 1:
+        settle(rows_all.at[:, pl.ds(0, fsdp_count - 1)], once.at[ROWS_SENT])
     for copy in backs:
         copy.wait_recv()
     for f in range(fsdp_count):
@@ -506,24 +530,34 @@
 
     for load in loads[6:9]:
         load.wait()
-    near = len(relative) // 2
-    chunks = [range(near), range(near, near + near // 2), range(near + near // 2, 2 * near)]
+
+    def unpack(t, chunk, at):
+        settle(arrived.at[t, pl.ds(0, sum(r > 0 for r in chunk))], xr.at[t, chunk_of[chunk[0]]])
+        for r in chunk:
+            block = arrived[t, r] if r > 0 else x_out[t, me // copies]
+            stacked[t, at:at + CAP, :thin] = block[:CAP, :]
+            stacked[t, at:at + CAP, thin:] = block[CAP:, :]
+            at += CAP
+
+    far_rows = near // 2 * CAP
+    for t in range(shares - 1):
+        unpack(t, chunks[0], 0)
+        x = stacked[t, :far_rows, :widths[t]]
+        begun[0] = jnp.dot(x, rows_of(t, gate), preferred_element_type=jnp.float32)
+        begun[1] = jnp.dot(x, rows_of(t, up), preferred_element_type=jnp.float32)
+    final = shares - 1
     for chunk in chunks:
+        first, count = far_first.index(chunk[0]) * CAP, len(chunk) * CAP
         g = u = 0.0
-        count = len(chunk) * CAP
         for t in range(shares):
-            for i, r in enumerate(chunk):
-                if r > 0:
-                    sends[t][r].wait_recv()
-                    block = arrived[t, r]
-                else:
-                    block = x_out[t, me // copies]
-                stacked[t, i * CAP:(i + 1) * CAP, :thin] = block[:CAP, :]
-                stacked[t, i * CAP:(i + 1) * CAP, thin:] = block[CAP:, :]
-            x = stacked[t, :count, :widths[t]]
+            if t < final and first < far_rows:
+                g, u = begun[0, first:first + count], begun[1, first:first + count]
+                continue
+            unpack(t, chunk, first)
+            x = stacked[t, first:first + count, :widths[t]]
             g = g + jnp.dot(x, rows_of(t, gate), preferred_element_type=jnp.float32)
             u = u + jnp.dot(x, rows_of(t, up), preferred_element_type=jnp.float32)
-        scales = stacked[shares - 1, :count, widths[-1]:widths[-1] + 2].astype(jnp.float32)
+        scales = stacked[final, first:first + count, widths[-1]:widths[-1] + 2].astype(jnp.float32)
         scales = scales[:, :1] + scales[:, 1:]
         g, u = g * scales, u * scales
         hidden = (g * jax.nn.sigmoid(1.702 * g) * (u + 1.0)).astype(jnp.bfloat16)
@@ -535,11 +569,8 @@
             target[CAP:] = right[i * CAP:(i + 1) * CAP, :]
             if r > 0:
                 returns[r].start()
-    for share in sends:
-        for copy in share.values():
-            copy.wait_send()
-    for copy in returns.values():
-        copy.wait_recv()
+    settle(arrived.at[:, pl.ds(0, seq_count - 1)], once.at[X_SENT])
+    settle(returned.at[pl.ds(0, seq_count - 1)], once.at[BACK_HERE])
     parts = jnp.dot(
         mix[...], returned[...].reshape(seq_count * 2 * CAP, fold), preferred_element_type=jnp.float32
     )
@@ -547,8 +578,7 @@
     stream = res[...].astype(jnp.float32) + out_ref[0].astype(jnp.float32)
     out_ref[1, :, :fold] = (stream[:, :fold] + mixed[0]).astype(jnp.bfloat16)
     out_ref[1, :, fold:] = (stream[:, fold:] + mixed[1][:, :D - fold]).astype(jnp.bfloat16)
-    for copy in returns.values():
-        copy.wait_send()
+    settle(returned.at[pl.ds(0, seq_count - 1)], once.at[BACK_SENT])
 
 
 def on_device(
@@ -609,20 +639,19 @@
             held(fsdp_count, rows, columns),
             held(shares, EXPERTS, 2 * CAP, thin),
             held(shares, seq_count, 2 * CAP, thin),
-            held(shares, seq_count // 2 * CAP, 2 * thin),
+            held(shares, seq_count * CAP, 2 * thin),
+            pltpu.VMEM((2, seq_count // 4 * CAP, gate_weight.shape[1]), jnp.float32),
             held(seq_count, 2 * CAP, fold),
             held(seq_count, 2 * CAP, fold),
             held(4 * rows, seq_count * 2 * CAP),
             held(EXPERTS * 2 * CAP, 2 * rows),
             dma((13,)),
         ]
-        + [dma((z_count,))] * 4
-        + [dma((2, z_count))] * 2
-        + [dma((2, 2, z_count, 3)), dma((2, z_count, 3)), dma((z_count, 3)), dma((z_count, 3))]
-        + [dma((2, z_count, 3))] * 2
-        + [dma((KVH, fsdp_count)), dma((KVH, fsdp_count)), dma((fsdp_count,)), dma((fsdp_count,))]
-        + [dma((shares, seq_count))] * 2
-        + [dma((seq_count,))] * 2,
+        + [dma((z_count,))] * 2
+        + [dma((z_count + 1, 4)), dma((z_count, 4)), dma((z_count, 3)), dma((z_count,))]
+        + [dma((KVH, 2, max(fsdp_count - 1, 1)))]
+        + [dma((fsdp_count,))] * 2
+        + [dma((shares, 3)), dma((9,))],
         compiler_params=pltpu.CompilerParams(
             collective_id=0, has_side_effects=True, vmem_limit_bytes=60 * 1024 * 1024
         ),

time: 66.8 us -> 66.4 us (level); the launches traced: 65.6 us -> 66.2 us
  no operation moved by 1% of the time
where the time goes in v4:
time: 66.4 us; the launch traced here: 66.2 us
  Pallas kernels  63.8 us (96%)
  local copies, waits for them, and re-layouts  1.79 us (3%)
    pallas_call x1, Pallas kernels, on_device(): pl.pallas_call(functools.partial(layer_kernel, seq_count, fsdp_count), ou...  63.8 us
    slice x1, local copies, waits for them, and re-layouts, on_device(): return (both[0][None], both[1][None])  1.79 us

profile of v4, /device:TPU:0, one launch (start us, length us, event | category | flops | bytes accessed | tf_op | source)
XLA Modules:
  0.0 66.2 jit_solution(5653926200959424355)
XLA Ops:
  0.6 63.8 %shard_map.140 = bf16[2,64,1440]{2,1,0:T(8,128)(2,1)} custom-call(f32[1,32]{1,0:T(1,128)} %bitcast.18, s32[1,32]{1,0:T(1,128)} %bitcast.19, bf16[1440]{0:T(1024)(128)(2,1)} %gain_hbm.1, s32[2,64]{1,0:T(2,128)} %bitcast.17, bf16[64,1440]{1,0:T(8,128)(2,1)} %bitcast.12, bf16[64,2048]{1,0:T(8,128)(2,1)} %bitcast.11, bf16[64,256]{1,0:T(8,128)(2,1)} %bitcast.15, ...), custom_call_target="tpu_custom_call" | custom-call | tf_op jit(solution)/shard_map/pallas_call | solution.py:615
  64.5 1.8 %fusion = (bf16[1,64,1440]{2,1,0:T(8,128)(2,1)}, bf16[1,64,1440]{2,1,0:T(8,128)(2,1)}) fusion(bf16[2,64,1440]{2,1,0:T(8,128)(2,1)} %shard_map.140), kind=kLoop, calls=%fused_computation | loop fusion | bytes 737280 | tf_op jit(solution)/shard_map/slice | solution.py:673
